TPU v7x, 32 devices: a whole 2x2x4 slice. The times are simulated.
32 devices in a mesh: row: 8 (over z, x), col: 4 (over y, core).
Axes of the slice: x: 2, y: 2, z: 4, core: 2. Of those that a mesh axis runs over, the one named last changes fastest.
Arguments:
- offsets: int32 [8, 4, 2], P('row', 'col'), may hold values from 1 to 3
- targets: float32 [3, 3, 256, 512], P(None, None, 'row', 'col'), may hold values from -60 to 60
- grid_fine: float32 [32, 256, 512], P(None, 'row', 'col'), may hold values from -6 to 6
- grid_coarse: float32 [32, 64, 128], P(None, 'row', 'col'), may hold values from -6 to 6
- weight_in: float32 [512, 64], replicated, may hold values from -0.75 to 0.75
- weight_mid: float32 [1, 512, 512], replicated, may hold values from -0.25 to 0.25
- weight_out: float32 [3, 512], replicated, may hold values from -0.397747564 to 0.397747564
- fine_first: float32 [32, 256, 512], P(None, 'row', 'col'), may hold values from -0.012 to 0.012
- fine_second: float32 [32, 256, 512], P(None, 'row', 'col'), may hold values from 1e-06 to 0.0001
- coarse_first: float32 [32, 64, 128], P(None, 'row', 'col'), may hold values from -0.012 to 0.012
- coarse_second: float32 [32, 64, 128], P(None, 'row', 'col'), may hold values from 1e-06 to 0.0001
- in_first: float32 [512, 64], replicated, may hold values from -0.012 to 0.012
- in_second: float32 [512, 64], replicated, may hold values from 1e-06 to 0.0001
- mid_first: float32 [1, 512, 512], replicated, may hold values from -0.012 to 0.012
- mid_second: float32 [1, 512, 512], replicated, may hold values from 1e-06 to 0.0001
- out_first: float32 [3, 512], replicated, may hold values from -0.012 to 0.012
- out_second: float32 [3, 512], replicated, may hold values from 1e-06 to 0.0001
Outputs:
- fine_step: float32 [32, 256, 512], P(None, 'row', 'col')
- coarse_step: float32 [32, 64, 128], P(None, 'row', 'col')
- input_step: float32 [512, 64], replicated
- middle_step: float32 [1, 512, 512], replicated
- output_step: float32 [3, 512], replicated
All inputs are finite; a program needn't handle non-finite values.
Results may differ from a plain program's by a relative error of at most 0.0014.
The roundings to bfloat16 on the way count: a program that leaves them out, or rounds other values in their place, can miss the bound.
Values sent between devices are 32-bit elements; how exact they have to be, the bound alone decides.
A program may use at most 64 MiB of HBM per device.

v0:
```python
import jax
import jax.numpy as jnp
from jax import lax
from jax.sharding import PartitionSpec as P

SUB = 4
RATIO = 4
ADAM_STEP = 10


BETA_ONE = 0.9
BETA_TWO = 0.99
ADAM_EPSILON = 1e-08
CLIP_RMS = 0.01
LOSS_VALUE = 0.25
MEAN_EPSILON = 1e-06


def shifted(block, axis, distance):
    devices = range(lax.axis_size(axis))
    route = [(i - distance, i) for i in devices if i - distance in devices]
    return lax.ppermute(block, axis, route)


def interp_table(samples, level_ratio, offset):
    positions = jnp.arange(samples, dtype=jnp.int32)
    base_index = positions // level_ratio
    fraction = (
        (positions % level_ratio).astype(jnp.float32) + offset.astype(jnp.float32) / SUB
    ) / level_ratio
    column = jnp.arange(samples // level_ratio + 1, dtype=jnp.int32)
    lower_hit = (column[None, :] == base_index[:, None]).astype(jnp.float32)
    upper_hit = (column[None, :] == base_index[:, None] + 1).astype(jnp.float32)
    return lower_hit * (1.0 - fraction)[:, None] + upper_hit * fraction[:, None]


def level_tables(row_count, col_count, shift_y, shift_x):
    return (
        interp_table(row_count, 1, shift_y),
        interp_table(col_count, 1, shift_x),
        interp_table(row_count, RATIO, shift_y),
        interp_table(col_count, RATIO, shift_x),
    )


def sample_level(extended, row_table, col_table):
    across = jnp.einsum("kjl,ml->kjm", extended, col_table, precision=lax.Precision.HIGHEST)
    return jnp.einsum("ij,kjm->kim", row_table, across, precision=lax.Precision.HIGHEST)


def spread_level(cotangent, row_table, col_table):
    backward = jnp.einsum("ij,kim->kjm", row_table, cotangent, precision=lax.Precision.HIGHEST)
    return jnp.einsum("kjm,ml->kjl", backward, col_table, precision=lax.Precision.HIGHEST)


def sample_features(fine_ext, coarse_ext, tables):
    fine_feat = sample_level(fine_ext, tables[0], tables[1])
    coarse_feat = sample_level(coarse_ext, tables[2], tables[3])
    channels, row_count, col_count = fine_feat.shape
    return jnp.concatenate(
        [
            fine_feat.reshape(channels, row_count * col_count),
            coarse_feat.reshape(channels, row_count * col_count),
        ],
        axis=0,
    ).astype(jnp.bfloat16)


def spread_features(feature_grad, tables):
    channels = feature_grad.shape[0] // 2
    row_count = tables[0].shape[0]
    col_count = tables[1].shape[0]
    fine_cot = feature_grad[:channels].reshape(channels, row_count, col_count)
    coarse_cot = feature_grad[channels:].reshape(channels, row_count, col_count)
    return (
        spread_level(fine_cot, tables[0], tables[1]),
        spread_level(coarse_cot, tables[2], tables[3]),
    )


def matmul(former, latter):
    return jnp.dot(former, latter, preferred_element_type=jnp.float32)


def contract_rows(former, latter):
    return lax.dot_general(
        former, latter, (((0,), (0,)), ((), ())), preferred_element_type=jnp.float32
    )


def contract_cols(former, latter):
    return lax.dot_general(
        former, latter, (((1,), (1,)), ((), ())), preferred_element_type=jnp.float32
    )


def silu_slope(pre_act):
    sigmoid = jax.nn.sigmoid(pre_act)
    return sigmoid * (1.0 + pre_act * (1.0 - sigmoid))


def decoder_forward(features, low_in, low_mid, low_out):
    pre_acts = [matmul(low_in, features)]
    activations = [jax.nn.silu(pre_acts[0]).astype(jnp.bfloat16)]
    pre_acts.append(matmul(low_mid[0], activations[-1]))
    activations.append(jax.nn.silu(pre_acts[-1]).astype(jnp.bfloat16))
    return (matmul(low_out, activations[-1]), pre_acts, activations)


def decoder_backward(features, pre_acts, activations, cotangent, low_in, low_mid, low_out):
    out_cotangent = cotangent.astype(jnp.bfloat16)
    grad_out = contract_cols(out_cotangent, activations[-1])
    upward = contract_rows(low_out, out_cotangent)
    grads_mid = []
    delta_low = (upward * silu_slope(pre_acts[1])).astype(jnp.bfloat16)
    grads_mid.insert(0, contract_cols(delta_low, activations[0]))
    upward = contract_rows(low_mid[0], delta_low)
    delta_low = (upward * silu_slope(pre_acts[0])).astype(jnp.bfloat16)
    grad_in = contract_cols(delta_low, features)
    feature_grad = contract_rows(low_in, delta_low)
    return (grad_in, jnp.stack(grads_mid), grad_out, feature_grad)


def pixel_cotangent(value_error, row_error, row_prior, col_error, col_prior):
    return (
        2.0 * LOSS_VALUE * value_error
        + 2.0 * (row_prior - row_error)
        + 2.0 * (col_prior - col_error)
    )


def clip_factor(total, entries):
    return jnp.minimum(1.0, CLIP_RMS / jnp.sqrt(total / entries + MEAN_EPSILON))


def adam_step(gradient, moment_one, moment_two, clip_scale):
    clipped = gradient * clip_scale
    new_one = BETA_ONE * moment_one + (1.0 - BETA_ONE) * clipped
    new_two = BETA_TWO * moment_two + (1.0 - BETA_TWO) * clipped * clipped
    return (
        new_one
        / (1.0 - BETA_ONE**ADAM_STEP)
        / (jnp.sqrt(new_two / (1.0 - BETA_TWO**ADAM_STEP)) + ADAM_EPSILON)
    )


def grid_total_sum(grid_local):
    return lax.psum(grid_local, ("row", "col"))


def shards(
    offsets,
    targets,
    grid_fine,
    grid_coarse,
    weight_in,
    weight_mid,
    weight_out,
    fine_first,
    fine_second,
    coarse_first,
    coarse_second,
    in_first,
    in_second,
    mid_first,
    mid_second,
    out_first,
    out_second,
):
    channels, sample_rows, sample_cols = grid_fine.shape
    coarse_rows = grid_coarse.shape[1]
    coarse_cols = grid_coarse.shape[2]
    low_in = weight_in.astype(jnp.bfloat16)
    low_mid = weight_mid.astype(jnp.bfloat16)
    low_out = weight_out.astype(jnp.bfloat16)
    top_rows = jnp.concatenate([grid_fine[:, :1, :], grid_coarse[:, :1, :]], axis=2)
    top_rows = shifted(top_rows, "row", -1)
    fine_tall = jnp.concatenate([grid_fine, top_rows[:, :, :sample_cols]], axis=1)
    coarse_tall = jnp.concatenate([grid_coarse, top_rows[:, :, sample_cols:]], axis=1)
    edge_cols = jnp.concatenate([fine_tall[:, :, :1], coarse_tall[:, :, :1]], axis=1)
    edge_cols = shifted(edge_cols, "col", -1)
    fine_ext = jnp.concatenate([fine_tall, edge_cols[:, : sample_rows + 1, :]], axis=2)
    coarse_ext = jnp.concatenate([coarse_tall, edge_cols[:, sample_rows + 1 :, :]], axis=2)
    tables = level_tables(sample_rows, sample_cols, offsets[0, 0, 0], offsets[0, 0, 1])
    features = sample_features(fine_ext, coarse_ext, tables)
    predicted, pre_acts, activations = decoder_forward(features, low_in, low_mid, low_out)
    outputs = predicted.shape[0]
    predicted = predicted.reshape(outputs, sample_rows, sample_cols)
    below = shifted(predicted[:, :1, :], "row", -1)
    beside = shifted(predicted[:, :, :1], "col", -1)
    row_global = lax.axis_index("row") * sample_rows + jnp.arange(sample_rows, dtype=jnp.int32)
    col_global = lax.axis_index("col") * sample_cols + jnp.arange(sample_cols, dtype=jnp.int32)
    row_valid = (row_global < lax.axis_size("row") * sample_rows - 1)[None, :, None]
    col_valid = (col_global < lax.axis_size("col") * sample_cols - 1)[None, None, :]
    row_next = jnp.concatenate([predicted[:, 1:, :], below], axis=1)
    col_next = jnp.concatenate([predicted[:, :, 1:], beside], axis=2)
    value_error = predicted - targets[0]
    row_error = jnp.where(row_valid, row_next - predicted - targets[1], 0.0)
    col_error = jnp.where(col_valid, col_next - predicted - targets[2], 0.0)
    above = shifted(row_error[:, -1:, :], "row", 1)
    before = shifted(col_error[:, :, -1:], "col", 1)
    row_prior = jnp.concatenate([above, row_error[:, :-1, :]], axis=1)
    col_prior = jnp.concatenate([before, col_error[:, :, :-1]], axis=2)
    cotangent = pixel_cotangent(value_error, row_error, row_prior, col_error, col_prior)
    grad_in, grad_mid, grad_out, feature_grad = decoder_backward(
        features,
        pre_acts,
        activations,
        cotangent.reshape(outputs, sample_rows * sample_cols),
        low_in,
        low_mid,
        low_out,
    )
    fine_back, coarse_back = spread_features(feature_grad, tables)
    side_cols = jnp.concatenate(
        [fine_back[:, :, sample_cols:], coarse_back[:, :, coarse_cols:]], axis=1
    )
    side_cols = shifted(side_cols, "col", 1)
    fine_tall_grad = jnp.concatenate(
        [fine_back[:, :, :1] + side_cols[:, : sample_rows + 1, :], fine_back[:, :, 1:sample_cols]],
        axis=2,
    )
    coarse_tall_grad = jnp.concatenate(
        [
            coarse_back[:, :, :1] + side_cols[:, sample_rows + 1 :, :],
            coarse_back[:, :, 1:coarse_cols],
        ],
        axis=2,
    )
    bottom_rows = jnp.concatenate(
        [fine_tall_grad[:, sample_rows:, :], coarse_tall_grad[:, coarse_rows:, :]], axis=2
    )
    bottom_rows = shifted(bottom_rows, "row", 1)
    fine_grad = jnp.concatenate(
        [
            fine_tall_grad[:, :1, :] + bottom_rows[:, :, :sample_cols],
            fine_tall_grad[:, 1:sample_rows, :],
        ],
        axis=1,
    )
    coarse_grad = jnp.concatenate(
        [
            coarse_tall_grad[:, :1, :] + bottom_rows[:, :, sample_cols:],
            coarse_tall_grad[:, 1:coarse_rows, :],
        ],
        axis=1,
    )
    grid_local = jnp.sum(fine_grad * fine_grad) + jnp.sum(coarse_grad * coarse_grad)
    devices = lax.axis_size("row") * lax.axis_size("col")
    grid_entries = (fine_grad.size + coarse_grad.size) * devices
    decoder_entries = weight_in.size + weight_mid.size + weight_out.size
    grad_in, grad_mid, grad_out = lax.psum((grad_in, grad_mid, grad_out), ("row", "col"))
    grid_total = grid_total_sum(grid_local)
    decoder_total = (
        jnp.sum(grad_in * grad_in) + jnp.sum(grad_mid * grad_mid) + jnp.sum(grad_out * grad_out)
    )
    decoder_scale = clip_factor(decoder_total, decoder_entries)
    middle_step = adam_step(grad_mid, mid_first, mid_second, decoder_scale)
    grid_scale = clip_factor(grid_total, grid_entries)
    fine_step = adam_step(fine_grad, fine_first, fine_second, grid_scale)
    coarse_step = adam_step(coarse_grad, coarse_first, coarse_second, grid_scale)
    input_step = adam_step(grad_in, in_first, in_second, decoder_scale)
    output_step = adam_step(grad_out, out_first, out_second, decoder_scale)
    return (fine_step, coarse_step, input_step, middle_step, output_step)


def solution(mesh):
    placed = (
        P("row", "col", None),
        P(None, None, "row", "col"),
        P(None, "row", "col"),
        P(None, "row", "col"),
        P(),
        P(),
        P(),
        P(None, "row", "col"),
        P(None, "row", "col"),
        P(None, "row", "col"),
        P(None, "row", "col"),
        P(),
        P(),
        P(),
        P(),
        P(),
        P(),
    )
    return jax.shard_map(
        shards,
        mesh=mesh,
        in_specs=placed,
        out_specs=(P(None, "row", "col"), P(None, "row", "col"), P(), P(), P()),
        check_vma=False,
    )
```

profile of v0, /device:TPU:0, one launch (start us, length us, event | category | flops | bytes accessed | tf_op | source)
XLA Modules:
  0.0 238.9 jit_solution(828096831755790455)
XLA Ops:
  10.5 1.3 fusion.148
  14.0 1.9 collective-permute-done
  19.1 1.8 collective-permute-done.1
  21.6 2.2 fusion.14
  26.9 4.4 %fusion.5 = (bf16[512,4096]{0,1:T(8,128)(2,1)S(1)}, f32[4096,512]{1,0:T(8,128)S(1)}) fusion(f32[1,512,512]{2,1,0:T(8,128)S(1)} %copy-done.11, f32[4096,512]{1,0:T(8,128)S(1)} %fusion.82), kind=kOutput, calls=%fused_computation.10 | convolution fusion | flops 2168717312 | bytes 22020096 | tf_op jit(solution)/shard_map/dot_general | solution.py:82
  35.3 3.6 %collective-permute-done.4 = f32[3,32,1]{2,1,0:T(8,128)S(1)} collective-permute-done((f32[3,32,1]{2,1,0:T(8,128)S(1)}, f32[3,32,1]{2,1,0:T(8,128)S(1)}, u32[]{:S(2)}, u32[]{:S(2)}) %collective-permute-start.4) | collective-permute-done | bytes 416 | tf_op jit(solution)/shard_map/ppermute | solution.py:22
  39.1 4.6 %collective-permute-start.5 = (f32[3,32,1]{2,1,0:T(8,128)S(1)}, f32[3,32,1]{2,1,0:T(8,128)S(1)}, u32[]{:S(2)}, u32[]{:S(2)}) collective-permute-start(f32[3,32,1]{2,1,0:T(8,128)S(1)} %slice.167), channel_id=1, source_target_pairs={{0,1},{1,2},{2,3},{4,5},{5,6},{6,7},{8,9},{9,10},{10,11},{12,13},{... | collective-permute-start | bytes 1160 | tf_op jit(solution)/shard_map/ppermute | solution.py:22
  43.8 5.1 %collective-permute-start.3 = (f32[3,1,128]{2,1,0:T(1,128)S(1)}, f32[3,1,128]{2,1,0:T(1,128)S(1)}, u32[]{:S(2)}, u32[]{:S(2)}) collective-permute-start(f32[3,1,128]{2,1,0:T(1,128)S(1)} %slice.163), channel_id=1, source_target_pairs={{0,4},{4,8},{8,12},{12,16},{16,20},{20,24},{24,28},{1,5},{5,9},{9,... | collective-permute-start | bytes 4616 | tf_op jit(solution)/shard_map/ppermute | solution.py:22
  50.3 3.5 %fusion.1 = bf16[512,4096]{0,1:T(8,128)(2,1)S(1)} fusion(f32[4096,512]{1,0:T(8,128)S(1)} %get-tuple-element.27, bf16[3,4096]{1,0:T(4,128)(2,1)S(1)} %fusion.63, f32[3,512]{1,0:T(4,128)S(1)} %copy-done.8), kind=kOutput, calls=%fused_computation.3 | convolution fusion | flops 31458816 | bytes 12613632 | tf_op jit(solution)/shard_map/dot_general | solution.py:86
  53.8 3.4 %convolution_bitcast_fusion.1 = f32[1,512,512]{2,1,0:T(8,128)} fusion(bf16[512,4096]{0,1:T(8,128)(2,1)S(1)} %fusion.1, f32[4096,512]{1,0:T(8,128)S(1)} %fusion.82), kind=kOutput, calls=%fused_computation.24 | convolution fusion | flops 2157969408 | bytes 13631488 | tf_op jit(solution)/shard_map/dot_general | solution.py:92
  57.3 3.6 %fusion = bf16[512,4096]{0,1:T(8,128)(2,1)S(1)} fusion(f32[4096,512]{1,0:T(8,128)S(1)} %fusion.82, bf16[512,4096]{0,1:T(8,128)(2,1)S(1)} %fusion.1, f32[1,512,512]{2,1,0:T(8,128)S(1)} %copy-done.11), kind=kOutput, calls=%fused_computation.1 | convolution fusion | flops 2166620160 | bytes 17825792 | tf_op jit(solution)/shard_map/dot_general | solution.py:86
  60.9 2.0 copy-done.1
  62.8 1.4 convolution_bitcast_fusion
  70.0 3.7 %fusion.150 = f32[512,64]{0,1:T(8,128)} fusion(bf16[64,4096]{1,0:T(8,128)(2,1)S(1)} %bitcast_dynamic-update-slice_fusion, bf16[512,4096]{0,1:T(8,128)(2,1)} %copy-done.1), kind=kOutput, calls=%fused_computation.235 | convolution fusion | flops 268435456 | bytes 4849664 | tf_op jit(solution)/shard_map/dot_general | solution.py:92
  76.6 4.9 %collective-permute-start.7 = (f32[32,1,160]{2,1,0:T(1,128)S(1)}, f32[32,1,160]{2,1,0:T(1,128)S(1)}, u32[]{:S(2)}, u32[]{:S(2)}) collective-permute-start(f32[32,1,160]{2,1,0:T(1,128)S(1)} %fusion.80), channel_id=1, source_target_pairs={{0,4},{4,8},{8,12},{12,16},{16,20},{20,24},{24,28},{1,5},{5,9},{9,... | collective-permute-start | bytes 61448 | tf_op jit(solution)/shard_map/ppermute | solution.py:22
  81.5 2.8 %fusion.149 = f32[3,512]{1,0:T(4,128)S(1)} fusion(bf16[3,4096]{1,0:T(4,128)(2,1)S(1)} %fusion.63, bf16[512,4096]{0,1:T(8,128)(2,1)} %copy-done), kind=kOutput, calls=%fused_computation.234 | convolution fusion | flops 12582912 | bytes 4225024 | tf_op jit(solution)/shard_map/dot_general | solution.py:92
  87.4 41.9 %all-reduce = (f32[]{:T(128)}, f32[3,512]{1,0:T(4,128)S(1)}) all-reduce(f32[]{:T(128)S(6)} %add.300, f32[3,512]{1,0:T(4,128)S(1)} %fusion.149), channel_id=1, replica_groups=mesh['row'=8,'col'=4] {'row','col'}, use_global_device_ids=true, to_apply=%region_2.3 | all-reduce | flops 1537 | bytes 12296 | tf_op jit(solution)/shard_map/psum | solution.py:148
  130.6 1.7 fusion.49
  132.3 2.5 %fusion.29 = f32[32,32,128]{2,1,0:T(8,128)} fusion(f32[32,32,128]{2,1,0:T(8,128)} %param.25, f32[32,32,128]{2,1,0:T(8,128)} %param.24, f32[]{:T(128)S(6)} %min.6, f32[32,33,127]{2,1,0:T(8,128)S(1)} %slice.175, f32[32,33,1]{2,1,0:T(8,128)S(1)} %copy.72, f32[32,1,128]{2,1,0:T(1,128)S(1)} %slice_add_fusion.1), kind=kLoop, calls=%fused_computation.47 | loop fusion | flops 2228224 | bytes 2129924 | tf_op jit(solution)/shard_map/div | solution.py:141
  134.7 86.2 %all-reduce.4.cloned.1.call-done = (f32[512,64]{0,1:T(8,128)}, f32[1,512,512]{2,1,0:T(8,128)}) async-done(((f32[512,64]{0,1:T(8,128)}, f32[1,512,512]{2,1,0:T(8,128)}), (f32[512,64]{0,1:T(8,128)}, f32[1,512,512]{2,1,0:T(8,128)})) %all-reduce.4.cloned.1.call-update) | async-done | bytes 1179664 | tf_op jit(solution)/shard_map/psum | solution.py:252
  220.9 2.1 multiply_reduce_fusion
  223.0 1.5 multiply_reduce_fusion.2
  227.2 3.2 %fusion.24 = f32[1,512,512]{2,1,0:T(8,128)} fusion(f32[1,512,512]{2,1,0:T(8,128)S(1)} %copy-done.2, f32[1,512,512]{2,1,0:T(8,128)} %get-tuple-element.8, f32[1,512,512]{2,1,0:T(8,128)} %param.30, f32[]{:T(128)S(6)} %min.7), kind=kLoop, calls=%fused_computation.39 | loop fusion | flops 3145728 | bytes 4194308 | tf_op jit(solution)/shard_map/div | solution.py:141
  230.4 1.7 fusion.54
  (105 shorter events, 28.2 us)
Async XLA Ops:
  7.2 18.5 %copy-start.3 = (f32[512,64]{0,1:T(8,128)S(1)}, f32[512,64]{0,1:T(8,128)}, u32[]{:S(2)}) copy-start(f32[512,64]{0,1:T(8,128)} %param.21) | copy-start | bytes 393220
  7.2 213.8 %all-reduce.4.cloned.1.call-start = ((), (), s32[]{:S(2)}) async-start(), calls=%async_computation | async-start | bytes 2359296 | tf_op jit(solution)/shard_map/psum | solution.py:252
  9.2 6.8 %collective-permute-start = (f32[32,1,160]{2,1,0:T(1,128)S(1)}, f32[32,1,160]{2,1,0:T(1,128)S(1)}, u32[]{:S(2)}, u32[]{:S(2)}) collective-permute-start(f32[32,1,160]{2,1,0:T(1,128)S(1)} %copy.60), channel_id=1, source_target_pairs={{4,0},{8,4},{12,8},{16,12},{20,16},{24,20},{28,24},{5,1},{9,5},{13... | collective-permute-start | bytes 61448 | tf_op jit(solution)/shard_map/ppermute | solution.py:22
  17.8 3.1 %collective-permute-start.1 = (f32[32,42,1]{1,0,2:T(8,128)S(1)}, f32[32,42,1]{1,0,2:T(8,128)S(1)}, u32[]{:S(2)}, u32[]{:S(2)}) collective-permute-start(f32[32,42,1]{1,0,2:T(8,128)S(1)} %pad_maximum_fusion.7), channel_id=1, source_target_pairs={{1,0},{2,1},{3,2},{5,4},{6,5},{7,6},{9,8},{10,9},{11,10},{13,12},{... | collective-permute-start | bytes 16136 | tf_op jit(solution)/shard_map/ppermute | solution.py:22
  23.8 3.1 %copy-start.11 = (f32[1,512,512]{2,1,0:T(8,128)S(1)}, f32[1,512,512]{2,1,0:T(8,128)}, u32[]{:S(2)}) copy-start(f32[1,512,512]{2,1,0:T(8,128)} %param.22) | copy-start | bytes 3145732
  26.9 4.4 %copy-start.8 = (f32[3,512]{1,0:T(4,128)S(1)}, f32[3,512]{1,0:T(4,128)}, u32[]{:S(2)}) copy-start(f32[3,512]{1,0:T(4,128)} %param.23) | copy-start | bytes 18436
  26.9 12.0 %copy-start.4 = (f32[3,3,32,128]{3,2,1,0:T(8,128)S(1)}, f32[3,3,32,128]{3,2,1,0:T(8,128)}, u32[]{:S(2)}) copy-start(f32[3,3,32,128]{3,2,1,0:T(8,128)} %param.18) | copy-start | bytes 442372
  31.4 22.5 %copy-start = (bf16[512,4096]{0,1:T(8,128)(2,1)}, bf16[512,4096]{0,1:T(8,128)(2,1)S(1)}, u32[]{:S(2)}) copy-start(bf16[512,4096]{0,1:T(8,128)(2,1)S(1)} %get-tuple-element.26) | copy-start | bytes 12582916
  32.6 6.4 %collective-permute-start.2 = (f32[3,1,128]{2,1,0:T(1,128)S(1)}, f32[3,1,128]{2,1,0:T(1,128)S(1)}, u32[]{:S(2)}, u32[]{:S(2)}) collective-permute-start(f32[3,1,128]{2,1,0:T(1,128)S(1)} %slice.162), channel_id=1, source_target_pairs={{4,0},{8,4},{12,8},{16,12},{20,16},{24,20},{28,24},{5,1},{9,5},{13... | collective-permute-start | bytes 4616 | tf_op jit(solution)/shard_map/ppermute | solution.py:22
  33.9 5.0 %collective-permute-start.4 = (f32[3,32,1]{2,1,0:T(8,128)S(1)}, f32[3,32,1]{2,1,0:T(8,128)S(1)}, u32[]{:S(2)}, u32[]{:S(2)}) collective-permute-start(f32[3,32,1]{2,1,0:T(8,128)S(1)} %bitcast.213), channel_id=1, source_target_pairs={{1,0},{2,1},{3,2},{5,4},{6,5},{7,6},{9,8},{10,9},{11,10},{13,12},{... | collective-permute-start | bytes 1160 | tf_op jit(solution)/shard_map/ppermute | solution.py:22
  39.1 9.8 %collective-permute-start.5 = (f32[3,32,1]{2,1,0:T(8,128)S(1)}, f32[3,32,1]{2,1,0:T(8,128)S(1)}, u32[]{:S(2)}, u32[]{:S(2)}) collective-permute-start(f32[3,32,1]{2,1,0:T(8,128)S(1)} %slice.167), channel_id=1, source_target_pairs={{0,1},{1,2},{2,3},{4,5},{5,6},{6,7},{8,9},{9,10},{10,11},{12,13},{... | collective-permute-start | bytes 1160 | tf_op jit(solution)/shard_map/ppermute | solution.py:22
  43.8 6.2 %collective-permute-start.3 = (f32[3,1,128]{2,1,0:T(1,128)S(1)}, f32[3,1,128]{2,1,0:T(1,128)S(1)}, u32[]{:S(2)}, u32[]{:S(2)}) collective-permute-start(f32[3,1,128]{2,1,0:T(1,128)S(1)} %slice.163), channel_id=1, source_target_pairs={{0,4},{4,8},{8,12},{12,16},{16,20},{20,24},{24,28},{1,5},{5,9},{9,... | collective-permute-start | bytes 4616 | tf_op jit(solution)/shard_map/ppermute | solution.py:22
  60.8 2.0 copy-start.1
  68.7 6.9 %collective-permute-start.6 = (f32[32,42,1]{1,0,2:T(8,128)S(1)}, f32[32,42,1]{1,0,2:T(8,128)S(1)}, u32[]{:S(2)}, u32[]{:S(2)}) collective-permute-start(f32[32,42,1]{1,0,2:T(8,128)S(1)} %pad_maximum_fusion.8), channel_id=1, source_target_pairs={{0,1},{1,2},{2,3},{4,5},{5,6},{6,7},{8,9},{9,10},{10,11},{12,13},{... | collective-permute-start | bytes 16136 | tf_op jit(solution)/shard_map/ppermute | solution.py:22
  73.6 57.0 %copy-start.5 = (f32[32,8,32]{2,1,0:T(8,128)S(1)}, f32[32,8,32]{2,1,0:T(8,128)}, u32[]{:S(2)}) copy-start(f32[32,8,32]{2,1,0:T(8,128)} %param.27) | copy-start | bytes 98308
  75.7 150.9 %copy-start.9 = (f32[3,512]{1,0:T(4,128)S(1)}, f32[3,512]{1,0:T(4,128)}, u32[]{:S(2)}) copy-start(f32[3,512]{1,0:T(4,128)} %param.33) | copy-start | bytes 18436
  75.7 150.9 %copy-start.10 = (f32[3,512]{1,0:T(4,128)S(1)}, f32[3,512]{1,0:T(4,128)}, u32[]{:S(2)}) copy-start(f32[3,512]{1,0:T(4,128)} %param.32) | copy-start | bytes 18436
  75.7 151.5 %copy-start.2 = (f32[1,512,512]{2,1,0:T(8,128)S(1)}, f32[1,512,512]{2,1,0:T(8,128)}, u32[]{:S(2)}) copy-start(f32[1,512,512]{2,1,0:T(8,128)} %param.31) | copy-start | bytes 3145732
  76.5 153.9 %copy-start.6 = (f32[512,64]{0,1:T(8,128)S(1)}, f32[512,64]{0,1:T(8,128)}, u32[]{:S(2)}) copy-start(f32[512,64]{0,1:T(8,128)} %param.29) | copy-start | bytes 393220
  76.5 153.8 %copy-start.7 = (f32[512,64]{0,1:T(8,128)S(1)}, f32[512,64]{0,1:T(8,128)}, u32[]{:S(2)}) copy-start(f32[512,64]{0,1:T(8,128)} %param.28) | copy-start | bytes 393220
  76.6 7.7 %collective-permute-start.7 = (f32[32,1,160]{2,1,0:T(1,128)S(1)}, f32[32,1,160]{2,1,0:T(1,128)S(1)}, u32[]{:S(2)}, u32[]{:S(2)}) collective-permute-start(f32[32,1,160]{2,1,0:T(1,128)S(1)} %fusion.80), channel_id=1, source_target_pairs={{0,4},{4,8},{8,12},{12,16},{16,20},{20,24},{24,28},{1,5},{5,9},{9,... | collective-permute-start | bytes 61448 | tf_op jit(solution)/shard_map/ppermute | solution.py:22
Sparse Core Ops, SparseCore 0:
  87.5 133.4 all-reduce.3
where the time goes:
time: 240 us; the launch traced here: 239 us
  waiting for transfers between devices  94.6 us (39%)
  blocking collectives  41.9 us (17%)
  matrix products  31.7 us (13%)
  starting transfers between devices  21.1 us (9%)
  between operations  19.8 us (8%)
  other arithmetic  17.7 us (7%)
  local copies, waits for them, and re-layouts  12.2 us (5%)
    psum x1, waiting for transfers between devices, shards(): lax.psum((grad_in, grad_mid, grad_out), ('row', 'col'))  86.2 us
    psum x1, blocking collectives, grid_total_sum(): return lax.psum(grid_local, ('row', 'col'))  41.9 us
    ppermute x8, starting transfers between devices, shifted(): return lax.ppermute(block, axis, route)  21.1 us
    dot_general x3, matrix products, contract_cols(): lax.dot_general(former, latter, (((1,), (1,)), ((), ())), preferred_eleme...  9.93 us
    div x5, other arithmetic, adam_step(): new_one / (1.0 - BETA_ONE ** ADAM_STEP)  9.62 us
    dot_general x3, matrix products, contract_rows(): lax.dot_general(former, latter, (((0,), (0,)), ((), ())), preferred_eleme...  8.45 us
    ppermute x8, waiting for transfers between devices, shifted(): return lax.ppermute(block, axis, route)  8.35 us
    dot_general x3, matrix products, matmul(): return jnp.dot(former, latter, preferred_element_type=jnp.float32)  6.85 us
  transfers between devices with their start and end apart: 9, of which 6 were waited for; matrix products, arithmetic and copies ran while one was open for 7% of the time, Pallas kernels for 0%

commit v1 on v0

--- a/solution.py
+++ b/solution.py
@@ -1,6 +1,8 @@
 import jax
 import jax.numpy as jnp
 from jax import lax
+from jax.experimental import pallas as pl
+from jax.experimental.pallas import tpu as pltpu
 from jax.sharding import PartitionSpec as P
 
 SUB = 4
@@ -144,8 +146,144 @@
     )
 
 
-def grid_total_sum(grid_local):
-    return lax.psum(grid_local, ("row", "col"))
+MESH = pl.DeviceIdType.MESH
+LANES = 128
+SUBLANES = 8
+
+
+def sum_kernel(
+    mine_ref, sum_ref, from_pair, paired, arrived, own, pair_send, pair_recv, send, recv
+):
+    row, col = lax.axis_index("row"), lax.axis_index("col")
+    chips = mine_ref.shape[1]
+    half_cols = lax.axis_size("col") // 2
+    core = lax.rem(col, 2)
+    chip = row * half_cols + lax.div(col, 2)
+    pair = (row, col + 1 - 2 * core)
+
+    def place(step):
+        other = lax.rem(chip + step, chips)
+        return other, (lax.div(other, half_cols), lax.rem(other, half_cols) * 2 + core)
+
+    def pair_copy(slot, source, target):
+        return pltpu.make_async_remote_copy(
+            src_ref=source,
+            dst_ref=target,
+            send_sem=pair_send.at[slot],
+            recv_sem=pair_recv.at[slot],
+            device_id=pair,
+            device_id_type=MESH,
+        )
+
+    def block_copy(step):
+        other, device = place(step)
+        return pltpu.make_async_remote_copy(
+            src_ref=paired.at[other],
+            dst_ref=arrived.at[step],
+            send_sem=send.at[0, step],
+            recv_sem=recv.at[0, step],
+            device_id=device,
+            device_id_type=MESH,
+        )
+
+    def result_copy(step):
+        _, device = place(step)
+        return pltpu.make_async_remote_copy(
+            src_ref=own,
+            dst_ref=sum_ref.at[core, chip],
+            send_sem=send.at[1, step],
+            recv_sem=recv.at[1, step],
+            device_id=device,
+            device_id_type=MESH,
+        )
+
+    barrier = pltpu.get_barrier_semaphore()
+    pl.semaphore_signal(barrier, inc=1, device_id=pair, device_id_type=MESH)
+
+    @pl.loop(1, chips)
+    def _(step):
+        _, device = place(step)
+        pl.semaphore_signal(barrier, inc=1, device_id=device, device_id_type=MESH)
+
+    pl.semaphore_wait(barrier, chips)
+
+    first = pair_copy(0, mine_ref.at[1 - core], from_pair)
+    first.start()
+    first.wait()
+
+    @pl.loop(1, chips)
+    def _(step):
+        other, _ = place(step)
+        paired[other] = mine_ref[core, other] + from_pair[other]
+        block_copy(step).start()
+
+    own[...] = mine_ref[core, chip] + from_pair[chip]
+
+    @pl.loop(1, chips)
+    def _(step):
+        block_copy(step).wait()
+        own[...] += arrived[step]
+
+    @pl.loop(1, chips)
+    def _(step):
+        result_copy(step).start()
+
+    sum_ref[core, chip] = own[...]
+
+    @pl.loop(1, chips)
+    def _(step):
+        result_copy(step).wait()
+
+    last = pair_copy(1, sum_ref.at[core], sum_ref.at[core])
+    last.start()
+    last.wait()
+
+
+def sum_over_devices(grad_in, grad_mid, grad_out, grid_local):
+    devices = lax.axis_size("row") * lax.axis_size("col")
+    chips = devices // 2
+    hidden, inputs = grad_in.shape
+    outputs = grad_out.shape[0]
+    used = hidden + inputs + outputs + 1
+    lanes = -(-used // LANES) * LANES
+    rows = -(-hidden // (devices * SUBLANES)) * SUBLANES
+    total_column = jnp.zeros((hidden, 1), jnp.float32).at[0, 0].set(grid_local)
+    packed = jnp.concatenate(
+        [
+            grad_mid[0],
+            grad_in,
+            grad_out.T,
+            total_column,
+            jnp.zeros((hidden, lanes - used), jnp.float32),
+        ],
+        axis=1,
+    )
+    packed = jnp.pad(packed, ((0, rows * devices - hidden), (0, 0)))
+    shape = (2, chips, rows, lanes)
+    summed = pl.pallas_call(
+        sum_kernel,
+        out_shape=jax.ShapeDtypeStruct(shape, jnp.float32),
+        in_specs=[pl.BlockSpec(memory_space=pltpu.VMEM)],
+        out_specs=pl.BlockSpec(memory_space=pltpu.VMEM),
+        scratch_shapes=[
+            pltpu.VMEM(shape[1:], jnp.float32),
+            pltpu.VMEM(shape[1:], jnp.float32),
+            pltpu.VMEM(shape[1:], jnp.float32),
+            pltpu.VMEM(shape[2:], jnp.float32),
+            pltpu.SemaphoreType.DMA((2,)),
+            pltpu.SemaphoreType.DMA((2,)),
+            pltpu.SemaphoreType.DMA((2, chips)),
+            pltpu.SemaphoreType.DMA((2, chips)),
+        ],
+        compiler_params=pltpu.CompilerParams(collective_id=0, has_side_effects=True),
+    )(packed.reshape(shape))
+    summed = summed.reshape(rows * devices, lanes)[:hidden]
+    return (
+        summed[:, hidden : hidden + inputs],
+        summed[:, :hidden][None],
+        summed[:, hidden + inputs : hidden + inputs + outputs].T,
+        summed[0, used - 1],
+    )
 
 
 def shards(
@@ -249,8 +387,9 @@
     devices = lax.axis_size("row") * lax.axis_size("col")
     grid_entries = (fine_grad.size + coarse_grad.size) * devices
     decoder_entries = weight_in.size + weight_mid.size + weight_out.size
-    grad_in, grad_mid, grad_out = lax.psum((grad_in, grad_mid, grad_out), ("row", "col"))
-    grid_total = grid_total_sum(grid_local)
+    grad_in, grad_mid, grad_out, grid_total = sum_over_devices(
+        grad_in, grad_mid, grad_out, grid_local
+    )
     decoder_total = (
         jnp.sum(grad_in * grad_in) + jnp.sum(grad_mid * grad_mid) + jnp.sum(grad_out * grad_out)
     )

time: 240 us -> 150 us (0.62)
  the two profiles are of different devices: /device:TPU:0 before, /device:TPU:27 now
where the time goes in v1:
time: 150 us; the launch traced here: 149 us
  Pallas kernels  44.7 us (30%)
  matrix products  31.6 us (21%)
  local copies, waits for them, and re-layouts  22.4 us (15%)
  starting transfers between devices  20.2 us (13%)
  other arithmetic  15.4 us (10%)
  waiting for transfers between devices  7.91 us (5%)
  between operations  6.63 us (4%)
    pallas_call x1, Pallas kernels, sum_over_devices(): pl.pallas_call(sum_kernel, out_shape=jax.ShapeDtypeStruct(shape, jnp.floa...  44.7 us
    ppermute x8, starting transfers between devices, shifted(): return lax.ppermute(block, axis, route)  20.2 us
    dot_general x3, matrix products, contract_cols(): lax.dot_general(former, latter, (((1,), (1,)), ((), ())), preferred_eleme...  9.36 us
    dot_general x3, matrix products, contract_rows(): lax.dot_general(former, latter, (((0,), (0,)), ((), ())), preferred_eleme...  8.46 us
    ppermute x8, waiting for transfers between devices, shifted(): return lax.ppermute(block, axis, route)  7.91 us
    unnamed x42, local copies, waits for them, and re-layouts  7.54 us
    dot_general x3, matrix products, matmul(): return jnp.dot(former, latter, preferred_element_type=jnp.float32)  7.28 us
    div x5, other arithmetic, adam_step(): new_one / (1.0 - BETA_ONE ** ADAM_STEP)  7.02 us
  transfers between devices with their start and end apart: 8, of which 5 were waited for; matrix products, arithmetic and copies ran while one was open for 6% of the time, Pallas kernels for 0%

profile of v1, /device:TPU:27, one launch (start us, length us, event | category | flops | bytes accessed | tf_op | source)
XLA Modules:
  0.0 148.8 jit_solution(7448333738776354278)
XLA Ops:
  2.6 2.2 %collective-permute-start = (f32[32,1,160]{2,1,0:T(1,128)S(1)}, f32[32,1,160]{2,1,0:T(1,128)S(1)}, u32[]{:S(2)}, u32[]{:S(2)}) collective-permute-start(f32[32,1,160]{2,1,0:T(1,128)S(1)} %copy.99), channel_id=1, source_target_pairs={{4,0},{8,4},{12,8},{16,12},{20,16},{24,20},{28,24},{5,1},{9,5},{13... | collective-permute-start | bytes 61448 | tf_op jit(solution)/shard_map/ppermute | solution.py:24
  10.2 2.9 %collective-permute-start.1 = (f32[32,42,1]{1,0,2:T(8,128)S(1)}, f32[32,42,1]{1,0,2:T(8,128)S(1)}, u32[]{:S(2)}, u32[]{:S(2)}) collective-permute-start(f32[32,42,1]{1,0,2:T(8,128)S(1)} %pad_maximum_fusion.7), channel_id=1, source_target_pairs={{1,0},{2,1},{3,2},{5,4},{6,5},{7,6},{9,8},{10,9},{11,10},{13,12},{... | collective-permute-start | bytes 16136 | tf_op jit(solution)/shard_map/ppermute | solution.py:24
  13.1 2.5 %collective-permute-done.1 = f32[32,42,1]{1,0,2:T(8,128)S(1)} collective-permute-done((f32[32,42,1]{1,0,2:T(8,128)S(1)}, f32[32,42,1]{1,0,2:T(8,128)S(1)}, u32[]{:S(2)}, u32[]{:S(2)}) %collective-permute-start.1) | collective-permute-done | bytes 5408 | tf_op jit(solution)/shard_map/ppermute | solution.py:24
  16.3 2.2 %fusion.14 = f32[32,33,128]{2,1,0:T(8,128)S(1)} fusion(f32[32,33,1]{2,1,0:T(8,128)S(1)} %copy.104, f32[32,1,128]{2,1,0:T(1,128)S(1)} %slice.189, f32[32,32,128]{2,1,0:T(8,128)} %param.21, f32[]{:T(128)} %bitcast.1, s32[128]{0:T(128)S(1)} %iota_add_fusion.1, f32[]{:T(128)S(6)} %sub.86), kind=kOutput, calls=%fused_computation.24 | convolution fusion | flops 209595072 | bytes 1086088 | tf_op jit(solution)/shard_map/kjl,ml->kjm/dot_general | solution.py:49
  20.4 2.5 %fusion.11 = (bf16[512,4096]{0,1:T(8,128)(2,1)S(1)}, f32[4096,512]{1,0:T(8,128)S(1)}) fusion(bf16[64,4096]{1,0:T(8,128)(2,1)S(1)} %bitcast_dynamic-update-slice_fusion, f32[512,64]{0,1:T(8,128)S(1)} %copy-done.9), kind=kOutput, calls=%fused_computation.19 | convolution fusion | flops 278953984 | bytes 13238272 | tf_op jit(solution)/shard_map/dot_general | solution.py:84
  22.9 3.6 %fusion.5 = (bf16[512,4096]{0,1:T(8,128)(2,1)S(1)}, f32[4096,512]{1,0:T(8,128)S(1)}) fusion(bf16[512,4096]{0,1:T(8,128)(2,1)S(1)} %get-tuple-element.54, f32[1,512,512]{2,1,0:T(8,128)S(1)} %copy-done.15), kind=kOutput, calls=%fused_computation.10 | convolution fusion | flops 2158231552 | bytes 17825792 | tf_op jit(solution)/shard_map/dot_general | solution.py:84
  26.5 1.9 %copy-done = bf16[512,4096]{0,1:T(8,128)(2,1)} copy-done((bf16[512,4096]{0,1:T(8,128)(2,1)}, bf16[512,4096]{0,1:T(8,128)(2,1)S(1)}, u32[]{:S(2)}) %copy-start) | copy-done | bytes 4194328
  29.7 1.9 %collective-permute-start.4 = (f32[3,32,1]{2,1,0:T(8,128)S(1)}, f32[3,32,1]{2,1,0:T(8,128)S(1)}, u32[]{:S(2)}, u32[]{:S(2)}) collective-permute-start(f32[3,32,1]{2,1,0:T(8,128)S(1)} %bitcast.246), channel_id=1, source_target_pairs={{1,0},{2,1},{3,2},{5,4},{6,5},{7,6},{9,8},{10,9},{11,10},{13,12},{... | collective-permute-start | bytes 1160 | tf_op jit(solution)/shard_map/ppermute | solution.py:24
  31.6 3.0 %collective-permute-start.2 = (f32[3,1,128]{2,1,0:T(1,128)S(1)}, f32[3,1,128]{2,1,0:T(1,128)S(1)}, u32[]{:S(2)}, u32[]{:S(2)}) collective-permute-start(f32[3,1,128]{2,1,0:T(1,128)S(1)} %slice.194), channel_id=1, source_target_pairs={{4,0},{8,4},{12,8},{16,12},{20,16},{24,20},{28,24},{5,1},{9,5},{13... | collective-permute-start | bytes 4616 | tf_op jit(solution)/shard_map/ppermute | solution.py:24
  35.5 4.5 %collective-permute-start.5 = (f32[3,32,1]{2,1,0:T(8,128)S(1)}, f32[3,32,1]{2,1,0:T(8,128)S(1)}, u32[]{:S(2)}, u32[]{:S(2)}) collective-permute-start(f32[3,32,1]{2,1,0:T(8,128)S(1)} %slice.199), channel_id=1, source_target_pairs={{0,1},{1,2},{2,3},{4,5},{5,6},{6,7},{8,9},{9,10},{10,11},{12,13},{... | collective-permute-start | bytes 1160 | tf_op jit(solution)/shard_map/ppermute | solution.py:24
  41.6 3.3 %collective-permute-done.3 = f32[3,1,128]{2,1,0:T(1,128)S(1)} collective-permute-done((f32[3,1,128]{2,1,0:T(1,128)S(1)}, f32[3,1,128]{2,1,0:T(1,128)S(1)}, u32[]{:S(2)}, u32[]{:S(2)}) %collective-permute-start.3) | collective-permute-done | bytes 1568 | tf_op jit(solution)/shard_map/ppermute | solution.py:24
  45.2 3.5 %fusion.1 = bf16[512,4096]{0,1:T(8,128)(2,1)S(1)} fusion(f32[4096,512]{1,0:T(8,128)S(1)} %get-tuple-element.57, bf16[3,4096]{1,0:T(4,128)(2,1)S(1)} %fusion.65, f32[3,512]{1,0:T(4,128)S(1)} %copy-done.14), kind=kOutput, calls=%fused_computation.3 | convolution fusion | flops 31458816 | bytes 12613632 | tf_op jit(solution)/shard_map/dot_general | solution.py:88
  48.7 3.3 %fusion.151 = f32[512,512]{0,1:T(8,128)} fusion(bf16[512,4096]{0,1:T(8,128)(2,1)S(1)} %fusion.1, bf16[512,4096]{0,1:T(8,128)(2,1)S(1)} %get-tuple-element.54), kind=kOutput, calls=%fused_computation.239 | convolution fusion | flops 2147483648 | bytes 9437184 | tf_op jit(solution)/shard_map/dot_general | solution.py:94
  52.0 3.6 %fusion = bf16[512,4096]{0,1:T(8,128)(2,1)S(1)} fusion(f32[4096,512]{1,0:T(8,128)S(1)} %get-tuple-element.55, bf16[512,4096]{0,1:T(8,128)(2,1)S(1)} %fusion.1, f32[1,512,512]{2,1,0:T(8,128)S(1)} %copy-done.15), kind=kOutput, calls=%fused_computation.1 | convolution fusion | flops 2166620160 | bytes 17825792 | tf_op jit(solution)/shard_map/dot_general | solution.py:88
  61.4 2.8 %collective-permute-start.6 = (f32[32,42,1]{1,0,2:T(8,128)S(1)}, f32[32,42,1]{1,0,2:T(8,128)S(1)}, u32[]{:S(2)}, u32[]{:S(2)}) collective-permute-start(f32[32,42,1]{1,0,2:T(8,128)S(1)} %pad_maximum_fusion.8), channel_id=1, source_target_pairs={{0,1},{1,2},{2,3},{4,5},{5,6},{6,7},{8,9},{9,10},{10,11},{12,13},{... | collective-permute-start | bytes 16136 | tf_op jit(solution)/shard_map/ppermute | solution.py:24
  64.2 3.2 %fusion.153 = f32[512,64]{0,1:T(8,128)S(1)} fusion(bf16[64,4096]{1,0:T(8,128)(2,1)} %copy-done.2, bf16[512,4096]{0,1:T(8,128)(2,1)} %copy-done.1), kind=kOutput, calls=%fused_computation.241 | convolution fusion | flops 268435456 | bytes 4849664 | tf_op jit(solution)/shard_map/dot_general | solution.py:94
  70.9 2.8 %fusion.152 = f32[512,3]{0,1:T(4,128)S(1)} fusion(bf16[512,4096]{0,1:T(8,128)(2,1)} %copy-done, bf16[3,4096]{1,0:T(4,128)(2,1)S(1)} %fusion.65), kind=kOutput, calls=%fused_computation.240 | convolution fusion | flops 12582912 | bytes 4225024 | tf_op jit(solution)/shard_map/dot_general | solution.py:94
  79.0 2.3 %concatenate.86 = f32[512,640]{0,1:T(8,128)S(1)} concatenate(f32[512,512]{0,1:T(8,128)} %fusion.151, f32[512,64]{0,1:T(8,128)S(1)} %fusion.153, f32[512,3]{0,1:T(4,128)S(1)} %fusion.152, f32[512,1]{0,1:T(1,128)S(1)} %scatter.4, f32[512,60]{0,1:T(8,128)S(1)} %broadcast_in_dim.77), dimensions={1} | concatenate | bytes 2621440 | tf_op jit(solution)/shard_map/concatenate | solution.py:251
  82.7 44.7 %shard_map.200 = f32[2,16,16,640]{3,2,1,0:T(8,128)} custom-call(f32[2,16,16,640]{3,2,1,0:T(8,128)} %bitcast.238), custom_call_target="tpu_custom_call" | custom-call | tf_op jit(solution)/shard_map/pallas_call | solution.py:263
  127.4 1.7 %slice.214 = f32[512,64]{1,0:T(8,128)} slice(f32[512,640]{1,0:T(8,128)} %bitcast.233), slice={[0:512], [512:576]} | slice | bytes 262144 | tf_op jit(solution)/shard_map/slice | solution.py:282
  129.1 2.1 %multiply_reduce_fusion = f32[]{:T(128)} fusion(f32[512,640]{1,0:T(8,128)} %bitcast.234), kind=kLoop, calls=%fused_computation.42 | loop fusion | flops 524287 | bytes 1048580 | tf_op jit(solution)/shard_map/reduce_sum | solution.py:394
  131.2 1.8 %slice.216 = f32[512,3]{1,0:T(8,128)} slice(f32[512,640]{1,0:T(8,128)} %bitcast.235), slice={[0:512], [576:579]} | slice | bytes 12288 | tf_op jit(solution)/shard_map/slice | solution.py:284
  135.9 1.7 %copy.123 = f32[512,3]{0,1:T(4,128)} copy(f32[512,3]{1,0:T(8,128)} %slice.216) | data formatting | bytes 12288
  143.1 2.9 %fusion.25 = f32[1,512,512]{2,1,0:T(8,128)} fusion(f32[1,512,512]{2,1,0:T(8,128)S(1)} %copy-done.3, f32[1,512,512]{2,1,0:T(8,128)S(1)} %copy-done.4, f32[512,640]{1,0:T(8,128)} %bitcast.237, f32[]{:T(128)S(6)} %min.7), kind=kLoop, calls=%fused_computation.39 | loop fusion | flops 3145728 | bytes 4194308 | tf_op jit(solution)/shard_map/div | solution.py:143
  (119 shorter events, 35.4 us)
Async XLA Ops:
  2.6 5.8 %collective-permute-start = (f32[32,1,160]{2,1,0:T(1,128)S(1)}, f32[32,1,160]{2,1,0:T(1,128)S(1)}, u32[]{:S(2)}, u32[]{:S(2)}) collective-permute-start(f32[32,1,160]{2,1,0:T(1,128)S(1)} %copy.99), channel_id=1, source_target_pairs={{4,0},{8,4},{12,8},{16,12},{20,16},{24,20},{28,24},{5,1},{9,5},{13... | collective-permute-start | bytes 61448 | tf_op jit(solution)/shard_map/ppermute | solution.py:24
  7.4 12.9 %copy-start.9 = (f32[512,64]{0,1:T(8,128)S(1)}, f32[512,64]{0,1:T(8,128)}, u32[]{:S(2)}) copy-start(f32[512,64]{0,1:T(8,128)} %param.23) | copy-start | bytes 393220
  10.2 5.4 %collective-permute-start.1 = (f32[32,42,1]{1,0,2:T(8,128)S(1)}, f32[32,42,1]{1,0,2:T(8,128)S(1)}, u32[]{:S(2)}, u32[]{:S(2)}) collective-permute-start(f32[32,42,1]{1,0,2:T(8,128)S(1)} %pad_maximum_fusion.7), channel_id=1, source_target_pairs={{1,0},{2,1},{3,2},{5,4},{6,5},{7,6},{9,8},{10,9},{11,10},{13,12},{... | collective-permute-start | bytes 16136 | tf_op jit(solution)/shard_map/ppermute | solution.py:24
  20.3 2.5 %copy-start.2 = (bf16[64,4096]{1,0:T(8,128)(2,1)}, bf16[64,4096]{1,0:T(8,128)(2,1)S(1)}, u32[]{:S(2)}) copy-start(bf16[64,4096]{1,0:T(8,128)(2,1)S(1)} %bitcast_dynamic-update-slice_fusion) | copy-start | bytes 1572868
  20.4 2.5 %copy-start.15 = (f32[1,512,512]{2,1,0:T(8,128)S(1)}, f32[1,512,512]{2,1,0:T(8,128)}, u32[]{:S(2)}) copy-start(f32[1,512,512]{2,1,0:T(8,128)} %param.24) | copy-start | bytes 3145732
  22.9 5.5 %copy-start.14 = (f32[3,512]{1,0:T(4,128)S(1)}, f32[3,512]{1,0:T(4,128)}, u32[]{:S(2)}) copy-start(f32[3,512]{1,0:T(4,128)} %param.25) | copy-start | bytes 18436
  26.5 1.9 %copy-start = (bf16[512,4096]{0,1:T(8,128)(2,1)}, bf16[512,4096]{0,1:T(8,128)(2,1)S(1)}, u32[]{:S(2)}) copy-start(bf16[512,4096]{0,1:T(8,128)(2,1)S(1)} %get-tuple-element.56) | copy-start | bytes 12582916
  26.5 8.8 %copy-start.8 = (f32[3,3,32,128]{3,2,1,0:T(8,128)S(1)}, f32[3,3,32,128]{3,2,1,0:T(8,128)}, u32[]{:S(2)}) copy-start(f32[3,3,32,128]{3,2,1,0:T(8,128)} %param.20) | copy-start | bytes 442372
  29.7 5.4 %collective-permute-start.4 = (f32[3,32,1]{2,1,0:T(8,128)S(1)}, f32[3,32,1]{2,1,0:T(8,128)S(1)}, u32[]{:S(2)}, u32[]{:S(2)}) collective-permute-start(f32[3,32,1]{2,1,0:T(8,128)S(1)} %bitcast.246), channel_id=1, source_target_pairs={{1,0},{2,1},{3,2},{5,4},{6,5},{7,6},{9,8},{10,9},{11,10},{13,12},{... | collective-permute-start | bytes 1160 | tf_op jit(solution)/shard_map/ppermute | solution.py:24
  31.6 3.7 %collective-permute-start.2 = (f32[3,1,128]{2,1,0:T(1,128)S(1)}, f32[3,1,128]{2,1,0:T(1,128)S(1)}, u32[]{:S(2)}, u32[]{:S(2)}) collective-permute-start(f32[3,1,128]{2,1,0:T(1,128)S(1)} %slice.194), channel_id=1, source_target_pairs={{4,0},{8,4},{12,8},{16,12},{20,16},{24,20},{28,24},{5,1},{9,5},{13... | collective-permute-start | bytes 4616 | tf_op jit(solution)/shard_map/ppermute | solution.py:24
  35.5 6.1 %collective-permute-start.5 = (f32[3,32,1]{2,1,0:T(8,128)S(1)}, f32[3,32,1]{2,1,0:T(8,128)S(1)}, u32[]{:S(2)}, u32[]{:S(2)}) collective-permute-start(f32[3,32,1]{2,1,0:T(8,128)S(1)} %slice.199), channel_id=1, source_target_pairs={{0,1},{1,2},{2,3},{4,5},{5,6},{6,7},{8,9},{9,10},{10,11},{12,13},{... | collective-permute-start | bytes 1160 | tf_op jit(solution)/shard_map/ppermute | solution.py:24
  40.1 4.9 %collective-permute-start.3 = (f32[3,1,128]{2,1,0:T(1,128)S(1)}, f32[3,1,128]{2,1,0:T(1,128)S(1)}, u32[]{:S(2)}, u32[]{:S(2)}) collective-permute-start(f32[3,1,128]{2,1,0:T(1,128)S(1)} %slice.195), channel_id=1, source_target_pairs={{0,4},{4,8},{8,12},{12,16},{16,20},{20,24},{24,28},{1,5},{5,9},{9,... | collective-permute-start | bytes 4616 | tf_op jit(solution)/shard_map/ppermute | solution.py:24
  55.6 2.0 %copy-start.1 = (bf16[512,4096]{0,1:T(8,128)(2,1)}, bf16[512,4096]{0,1:T(8,128)(2,1)S(1)}, u32[]{:S(2)}) copy-start(bf16[512,4096]{0,1:T(8,128)(2,1)S(1)} %fusion) | copy-start | bytes 12582916
  61.4 7.1 %collective-permute-start.6 = (f32[32,42,1]{1,0,2:T(8,128)S(1)}, f32[32,42,1]{1,0,2:T(8,128)S(1)}, u32[]{:S(2)}, u32[]{:S(2)}) collective-permute-start(f32[32,42,1]{1,0,2:T(8,128)S(1)} %pad_maximum_fusion.8), channel_id=1, source_target_pairs={{0,1},{1,2},{2,3},{4,5},{5,6},{6,7},{8,9},{9,10},{10,11},{12,13},{... | collective-permute-start | bytes 16136 | tf_op jit(solution)/shard_map/ppermute | solution.py:24
  69.4 5.8 %collective-permute-start.7 = (f32[32,1,160]{2,1,0:T(1,128)S(1)}, f32[32,1,160]{2,1,0:T(1,128)S(1)}, u32[]{:S(2)}, u32[]{:S(2)}) collective-permute-start(f32[32,1,160]{2,1,0:T(1,128)S(1)} %fusion.82), channel_id=1, source_target_pairs={{0,4},{4,8},{8,12},{12,16},{16,20},{20,24},{24,28},{1,5},{5,9},{9,... | collective-permute-start | bytes 61448 | tf_op jit(solution)/shard_map/ppermute | solution.py:24
  82.7 60.4 %copy-start.3 = (f32[1,512,512]{2,1,0:T(8,128)S(1)}, f32[1,512,512]{2,1,0:T(8,128)}, u32[]{:S(2)}) copy-start(f32[1,512,512]{2,1,0:T(8,128)} %param.33) | copy-start | bytes 3145732
  82.7 60.4 %copy-start.4 = (f32[1,512,512]{2,1,0:T(8,128)S(1)}, f32[1,512,512]{2,1,0:T(8,128)}, u32[]{:S(2)}) copy-start(f32[1,512,512]{2,1,0:T(8,128)} %param.32) | copy-start | bytes 3145732
  140.9 5.1 %copy-start.10 = (f32[512,64]{0,1:T(8,128)S(1)}, f32[512,64]{0,1:T(8,128)}, u32[]{:S(2)}) copy-start(f32[512,64]{0,1:T(8,128)} %param.31) | copy-start | bytes 393220
  140.9 5.1 %copy-start.11 = (f32[512,64]{0,1:T(8,128)S(1)}, f32[512,64]{0,1:T(8,128)}, u32[]{:S(2)}) copy-start(f32[512,64]{0,1:T(8,128)} %param.30) | copy-start | bytes 393220
  140.9 5.9 %copy-start.5 = (f32[32,32,128]{2,1,0:T(8,128)S(1)}, f32[32,32,128]{2,1,0:T(8,128)}, u32[]{:S(2)}) copy-start(f32[32,32,128]{2,1,0:T(8,128)} %param.27) | copy-start | bytes 1572868
  140.9 5.9 %copy-start.6 = (f32[32,32,128]{2,1,0:T(8,128)S(1)}, f32[32,32,128]{2,1,0:T(8,128)}, u32[]{:S(2)}) copy-start(f32[32,32,128]{2,1,0:T(8,128)} %param.26) | copy-start | bytes 1572868
  140.9 7.1 %copy-start.7 = (f32[32,8,32]{2,1,0:T(8,128)S(1)}, f32[32,8,32]{2,1,0:T(8,128)}, u32[]{:S(2)}) copy-start(f32[32,8,32]{2,1,0:T(8,128)} %get-tuple-element.38) | copy-start | bytes 98308
  140.9 7.1 %copy-start.12 = (f32[32,8,32]{2,1,0:T(8,128)S(1)}, f32[32,8,32]{2,1,0:T(8,128)}, u32[]{:S(2)}) copy-start(f32[32,8,32]{2,1,0:T(8,128)} %param.29) | copy-start | bytes 98308
  141.0 7.1 %copy-start.13 = (f32[32,8,32]{2,1,0:T(8,128)S(1)}, f32[32,8,32]{2,1,0:T(8,128)}, u32[]{:S(2)}) copy-start(f32[32,8,32]{2,1,0:T(8,128)} %param.28) | copy-start | bytes 98308

commit v2 on v1

--- a/solution.py
+++ b/solution.py
@@ -1,3 +1,5 @@
+import functools
+
 import jax
 import jax.numpy as jnp
 from jax import lax
@@ -151,8 +153,27 @@
 SUBLANES = 8
 
 
-def sum_kernel(
-    mine_ref, sum_ref, from_pair, paired, arrived, own, pair_send, pair_recv, send, recv
+def decoder_kernel(
+    used,
+    mid_ref,
+    rest_ref,
+    mid_first_ref,
+    mid_second_ref,
+    rest_first_ref,
+    rest_second_ref,
+    mid_step_ref,
+    rest_step_ref,
+    total_ref,
+    mine_ref,
+    sum_ref,
+    from_pair,
+    paired,
+    arrived,
+    own,
+    pair_send,
+    pair_recv,
+    send,
+    recv,
 ):
     row, col = lax.axis_index("row"), lax.axis_index("col")
     chips = mine_ref.shape[1]
@@ -205,6 +226,19 @@
         _, device = place(step)
         pl.semaphore_signal(barrier, inc=1, device_id=device, device_id_type=MESH)
 
+    hidden, mids = mid_ref.shape
+    rows, lanes = mine_ref.shape[2:]
+    rests = lanes - mids
+    blocks = hidden // rows
+    for block in range(2 * chips):
+        where = divmod(block, chips)
+        if block < blocks:
+            span = slice(block * rows, (block + 1) * rows)
+            mine_ref[where[0], where[1], :, :mids] = mid_ref[span, :]
+            mine_ref[where[0], where[1], :, mids:] = rest_ref[span, :]
+        else:
+            mine_ref[where[0], where[1]] = jnp.zeros((rows, lanes), jnp.float32)
+
     pl.semaphore_wait(barrier, chips)
 
     first = pair_copy(0, mine_ref.at[1 - core], from_pair)
@@ -238,34 +272,61 @@
     last.start()
     last.wait()
 
-
-def sum_over_devices(grad_in, grad_mid, grad_out, grid_local):
+    total_ref[...] = sum_ref[0, 0, :SUBLANES, mids:]
+    kept = lax.broadcasted_iota(jnp.int32, (rows, rests), 1) < used
+    mid_squares = jnp.zeros((rows, mids), jnp.float32)
+    rest_squares = jnp.zeros((rows, rests), jnp.float32)
+    for block in range(blocks):
+        where = divmod(block, chips)
+        mid = sum_ref[where[0], where[1], :, :mids]
+        rest = sum_ref[where[0], where[1], :, mids:]
+        mid_squares += mid * mid
+        rest_squares += jnp.where(kept, rest * rest, 0.0)
+    total = jnp.sum(mid_squares, keepdims=True) + jnp.sum(rest_squares, keepdims=True)
+    scale = clip_factor(total, hidden * (mids + used))
+    for block in range(blocks):
+        where = divmod(block, chips)
+        span = slice(block * rows, (block + 1) * rows)
+        mid_step_ref[span, :] = adam_step(
+            sum_ref[where[0], where[1], :, :mids],
+            mid_first_ref[span, :],
+            mid_second_ref[span, :],
+            scale,
+        )
+        rest_step_ref[span, :] = adam_step(
+            sum_ref[where[0], where[1], :, mids:],
+            rest_first_ref[span, :],
+            rest_second_ref[span, :],
+            scale,
+        )
+
+
+def decoder_steps(gradients, firsts, seconds, grid_local):
+    grad_in, grad_mid, grad_out = gradients
     devices = lax.axis_size("row") * lax.axis_size("col")
     chips = devices // 2
     hidden, inputs = grad_in.shape
     outputs = grad_out.shape[0]
-    used = hidden + inputs + outputs + 1
-    lanes = -(-used // LANES) * LANES
+    mids = grad_mid.shape[2]
+    used = inputs + outputs
+    rests = -(-(used + 1) // LANES) * LANES
     rows = -(-hidden // (devices * SUBLANES)) * SUBLANES
-    total_column = jnp.zeros((hidden, 1), jnp.float32).at[0, 0].set(grid_local)
-    packed = jnp.concatenate(
-        [
-            grad_mid[0],
-            grad_in,
-            grad_out.T,
-            total_column,
-            jnp.zeros((hidden, lanes - used), jnp.float32),
-        ],
-        axis=1,
-    )
-    packed = jnp.pad(packed, ((0, rows * devices - hidden), (0, 0)))
-    shape = (2, chips, rows, lanes)
-    summed = pl.pallas_call(
-        sum_kernel,
-        out_shape=jax.ShapeDtypeStruct(shape, jnp.float32),
-        in_specs=[pl.BlockSpec(memory_space=pltpu.VMEM)],
-        out_specs=pl.BlockSpec(memory_space=pltpu.VMEM),
+
+    def beside(block_in, block_out, fill):
+        column = jnp.full((hidden, rests - used), fill, jnp.float32)
+        return jnp.concatenate([block_in, block_out.T, column], axis=1)
+
+    shape = (2, chips, rows, mids + rests)
+    flat = jax.ShapeDtypeStruct((hidden, mids), jnp.float32)
+    side = jax.ShapeDtypeStruct((hidden, rests), jnp.float32)
+    mid_step, rest_step, total = pl.pallas_call(
+        functools.partial(decoder_kernel, used),
+        out_shape=(flat, side, jax.ShapeDtypeStruct((SUBLANES, rests), jnp.float32)),
+        in_specs=[pl.BlockSpec(memory_space=pltpu.VMEM)] * 6,
+        out_specs=(pl.BlockSpec(memory_space=pltpu.VMEM),) * 3,
         scratch_shapes=[
+            pltpu.VMEM(shape, jnp.float32),
+            pltpu.VMEM(shape, jnp.float32),
             pltpu.VMEM(shape[1:], jnp.float32),
             pltpu.VMEM(shape[1:], jnp.float32),
             pltpu.VMEM(shape[1:], jnp.float32),
@@ -276,13 +337,19 @@
             pltpu.SemaphoreType.DMA((2, chips)),
         ],
         compiler_params=pltpu.CompilerParams(collective_id=0, has_side_effects=True),
-    )(packed.reshape(shape))
-    summed = summed.reshape(rows * devices, lanes)[:hidden]
+    )(
+        grad_mid[0],
+        beside(grad_in, grad_out, grid_local),
+        firsts[1][0],
+        seconds[1][0],
+        beside(firsts[0], firsts[2], 0.0),
+        beside(seconds[0], seconds[2], 1.0),
+    )
     return (
-        summed[:, hidden : hidden + inputs],
-        summed[:, :hidden][None],
-        summed[:, hidden + inputs : hidden + inputs + outputs].T,
-        summed[0, used - 1],
+        rest_step[:, :inputs],
+        mid_step[None],
+        rest_step[:, inputs:used].T,
+        total[0, used],
     )
 
 
@@ -326,6 +393,10 @@
     predicted = predicted.reshape(outputs, sample_rows, sample_cols)
     below = shifted(predicted[:, :1, :], "row", -1)
     beside = shifted(predicted[:, :, :1], "col", -1)
+    above = jnp.concatenate([predicted[:, -1:, :], targets[1][:, -1:, :]], axis=0)
+    above = shifted(above, "row", 1)
+    before = jnp.concatenate([predicted[:, :, -1:], targets[2][:, :, -1:]], axis=0)
+    before = shifted(before, "col", 1)
     row_global = lax.axis_index("row") * sample_rows + jnp.arange(sample_rows, dtype=jnp.int32)
     col_global = lax.axis_index("col") * sample_cols + jnp.arange(sample_cols, dtype=jnp.int32)
     row_valid = (row_global < lax.axis_size("row") * sample_rows - 1)[None, :, None]
@@ -335,8 +406,12 @@
     value_error = predicted - targets[0]
     row_error = jnp.where(row_valid, row_next - predicted - targets[1], 0.0)
     col_error = jnp.where(col_valid, col_next - predicted - targets[2], 0.0)
-    above = shifted(row_error[:, -1:, :], "row", 1)
-    before = shifted(col_error[:, :, -1:], "col", 1)
+    above = jnp.where(
+        lax.axis_index("row") > 0, predicted[:, :1, :] - above[:outputs] - above[outputs:], 0.0
+    )
+    before = jnp.where(
+        lax.axis_index("col") > 0, predicted[:, :, :1] - before[:outputs] - before[outputs:], 0.0
+    )
     row_prior = jnp.concatenate([above, row_error[:, :-1, :]], axis=1)
     col_prior = jnp.concatenate([before, col_error[:, :, :-1]], axis=2)
     cotangent = pixel_cotangent(value_error, row_error, row_prior, col_error, col_prior)
@@ -386,20 +461,15 @@
     grid_local = jnp.sum(fine_grad * fine_grad) + jnp.sum(coarse_grad * coarse_grad)
     devices = lax.axis_size("row") * lax.axis_size("col")
     grid_entries = (fine_grad.size + coarse_grad.size) * devices
-    decoder_entries = weight_in.size + weight_mid.size + weight_out.size
-    grad_in, grad_mid, grad_out, grid_total = sum_over_devices(
-        grad_in, grad_mid, grad_out, grid_local
-    )
-    decoder_total = (
-        jnp.sum(grad_in * grad_in) + jnp.sum(grad_mid * grad_mid) + jnp.sum(grad_out * grad_out)
-    )
-    decoder_scale = clip_factor(decoder_total, decoder_entries)
-    middle_step = adam_step(grad_mid, mid_first, mid_second, decoder_scale)
+    input_step, middle_step, output_step, grid_total = decoder_steps(
+        (grad_in, grad_mid, grad_out),
+        (in_first, mid_first, out_first),
+        (in_second, mid_second, out_second),
+        grid_local,
+    )
     grid_scale = clip_factor(grid_total, grid_entries)
     fine_step = adam_step(fine_grad, fine_first, fine_second, grid_scale)
     coarse_step = adam_step(coarse_grad, coarse_first, coarse_second, grid_scale)
-    input_step = adam_step(grad_in, in_first, in_second, decoder_scale)
-    output_step = adam_step(grad_out, out_first, out_second, decoder_scale)
     return (fine_step, coarse_step, input_step, middle_step, output_step)
 
 

time: 150 us -> 147 us (0.980)
  other arithmetic: 15.4 us -> 7.81 us
  matrix products: 31.6 us -> 36.9 us
  between operations: 6.63 us -> 4.54 us
  Pallas kernels: 44.7 us -> 46.6 us
  starting transfers between devices: 20.2 us -> 21.9 us
    unnamed x42 -> x47, local copies, waits for them, and re-layouts: 7.54 us -> 12 us
    reduce_sum x3 -> x0, other arithmetic: 4.06 us -> none  [the longest x1 2.12 us: shards(): jnp.sum(grad_mid * grad_mid)]
    div x5 -> x2, other arithmetic: 7.02 us -> 3.06 us  [adam_step(): new_one / (1.0 - BETA_ONE ** ADAM_STEP)]
    concatenate x2 -> x3, local copies, waits for them, and re-layouts: 3.76 us -> 0.23 us  [beside(): return jnp.concatenate([block_in, block_out.T, column], axis=1)]
    slice x6 -> x5, local copies, waits for them, and re-layouts: 4.8 us -> 1.52 us  [the longest x1 1.34 us: decoder_steps(): total[0, used]]
    dot_general x3, matrix products: 7.28 us -> 10.4 us  [matmul(): return jnp.dot(former, latter, preferred_element_type=jnp.float32)]
    dot_general x3, matrix products: 8.46 us -> 10.7 us  [contract_rows(): lax.dot_general(former, latter, (((0,), (0,)), ((), ())), preferred_eleme...]
    pallas_call x1, Pallas kernels: 44.7 us -> 46.6 us  [decoder_steps(): pl.pallas_call(functools.partial(decoder_kernel, used), out_shape=(flat,...]
  transfers between devices with their start and end apart: 8 -> 8, of which waited for: 5 -> 5; matrix products, arithmetic and copies ran while one was open for 6% -> 11% of each run, Pallas kernels for 0% -> 0%
where the time goes in v2:
time: 147 us
  Pallas kernels  46.6 us (32%)
  matrix products  36.9 us (25%)
  starting transfers between devices  21.9 us (15%)
  local copies, waits for them, and re-layouts  21.1 us (14%)
  other arithmetic  7.81 us (5%)
  waiting for transfers between devices  7.59 us (5%)
  between operations  4.54 us (3%)
    pallas_call x1, Pallas kernels, decoder_steps(): pl.pallas_call(functools.partial(decoder_kernel, used), out_shape=(flat,...  46.6 us
    ppermute x8, starting transfers between devices, shifted(): return lax.ppermute(block, axis, route)  21.9 us
    unnamed x47, local copies, waits for them, and re-layouts  12 us
    dot_general x3, matrix products, contract_rows(): lax.dot_general(former, latter, (((0,), (0,)), ((), ())), preferred_eleme...  10.7 us
    dot_general x3, matrix products, matmul(): return jnp.dot(former, latter, preferred_element_type=jnp.float32)  10.4 us
    dot_general x3, matrix products, contract_cols(): lax.dot_general(former, latter, (((1,), (1,)), ((), ())), preferred_eleme...  10.4 us
    ppermute x8, waiting for transfers between devices, shifted(): return lax.ppermute(block, axis, route)  7.59 us
    div x2, other arithmetic, adam_step(): new_one / (1.0 - BETA_ONE ** ADAM_STEP)  3.06 us
  transfers between devices with their start and end apart: 8, of which 5 were waited for; matrix products, arithmetic and copies ran while one was open for 11% of the time, Pallas kernels for 0%

profile of v2, /device:TPU:27, one launch (start us, length us, event | category | flops | bytes accessed | tf_op | source)
XLA Modules:
  0.0 146.6 jit_solution(7748040078427254759)
XLA Ops:
  2.6 2.2 %collective-permute-start = (f32[32,1,160]{2,1,0:T(1,128)S(1)}, f32[32,1,160]{2,1,0:T(1,128)S(1)}, u32[]{:S(2)}, u32[]{:S(2)}) collective-permute-start(f32[32,1,160]{2,1,0:T(1,128)S(1)} %copy.103), channel_id=1, source_target_pairs={{4,0},{8,4},{12,8},{16,12},{20,16},{24,20},{28,24},{5,1},{9,5},{13... | collective-permute-start | bytes 61448 | tf_op jit(solution)/shard_map/ppermute | solution.py:26
  4.8 1.3 fusion.134
  14.2 2.9 %collective-permute-start.1 = (f32[32,42,1]{1,0,2:T(8,128)S(1)}, f32[32,42,1]{1,0,2:T(8,128)S(1)}, u32[]{:S(2)}, u32[]{:S(2)}) collective-permute-start(f32[32,42,1]{1,0,2:T(8,128)S(1)} %pad_maximum_fusion.7), channel_id=1, source_target_pairs={{1,0},{2,1},{3,2},{5,4},{6,5},{7,6},{9,8},{10,9},{11,10},{13,12},{... | collective-permute-start | bytes 16136 | tf_op jit(solution)/shard_map/ppermute | solution.py:26
  17.1 2.4 %collective-permute-done.1 = f32[32,42,1]{1,0,2:T(8,128)S(1)} collective-permute-done((f32[32,42,1]{1,0,2:T(8,128)S(1)}, f32[32,42,1]{1,0,2:T(8,128)S(1)}, u32[]{:S(2)}, u32[]{:S(2)}) %collective-permute-start.1) | collective-permute-done | bytes 5408 | tf_op jit(solution)/shard_map/ppermute | solution.py:26
  23.3 4.6 %fusion.11 = (bf16[512,4096]{0,1:T(8,128)(2,1)S(1)}, f32[4096,512]{1,0:T(8,128)}) fusion(bf16[64,4096]{1,0:T(8,128)(2,1)S(1)} %bitcast_dynamic-update-slice_fusion, f32[512,64]{0,1:T(8,128)S(1)} %copy-done.7), kind=kOutput, calls=%fused_computation.19 | convolution fusion | flops 278953984 | bytes 13238272 | tf_op jit(solution)/shard_map/dot_general | solution.py:86
  27.9 4.6 %fusion.5 = (bf16[512,4096]{0,1:T(8,128)(2,1)S(1)}, f32[4096,512]{1,0:T(8,128)}) fusion(bf16[512,4096]{0,1:T(8,128)(2,1)S(1)} %get-tuple-element.50, f32[1,512,512]{2,1,0:T(8,128)S(1)} %copy-done.13), kind=kOutput, calls=%fused_computation.10 | convolution fusion | flops 2158231552 | bytes 17825792 | tf_op jit(solution)/shard_map/dot_general | solution.py:86
  32.6 2.0 %copy-done.2 = bf16[512,4096]{0,1:T(8,128)(2,1)} copy-done((bf16[512,4096]{0,1:T(8,128)(2,1)}, bf16[512,4096]{0,1:T(8,128)(2,1)S(1)}, u32[]{:S(2)}) %copy-start.2) | copy-done | bytes 4194328
  35.8 1.9 %collective-permute-start.4 = (f32[6,32,1]{2,1,0:T(8,128)S(1)}, f32[6,32,1]{2,1,0:T(8,128)S(1)}, u32[]{:S(2)}, u32[]{:S(2)}) collective-permute-start(f32[6,32,1]{2,1,0:T(8,128)S(1)} %pad_maximum_fusion.2), channel_id=1, source_target_pairs={{0,1},{1,2},{2,3},{4,5},{5,6},{6,7},{8,9},{9,10},{10,11},{12,13},{... | collective-permute-start | bytes 2312 | tf_op jit(solution)/shard_map/ppermute | solution.py:26
  37.9 1.5 %collective-permute-done.4 = f32[6,32,1]{2,1,0:T(8,128)S(1)} collective-permute-done((f32[6,32,1]{2,1,0:T(8,128)S(1)}, f32[6,32,1]{2,1,0:T(8,128)S(1)}, u32[]{:S(2)}, u32[]{:S(2)}) %collective-permute-start.4) | collective-permute-done | bytes 800 | tf_op jit(solution)/shard_map/ppermute | solution.py:26
  39.4 1.9 %collective-permute-start.5 = (f32[3,32,1]{2,1,0:T(8,128)S(1)}, f32[3,32,1]{2,1,0:T(8,128)S(1)}, u32[]{:S(2)}, u32[]{:S(2)}) collective-permute-start(f32[3,32,1]{2,1,0:T(8,128)S(1)} %get-tuple-element.47), channel_id=1, source_target_pairs={{1,0},{2,1},{3,2},{5,4},{6,5},{7,6},{9,8},{10,9},{11,10},{13,12},{... | collective-permute-start | bytes 1160 | tf_op jit(solution)/shard_map/ppermute | solution.py:26
  42.7 3.0 %collective-permute-done.5 = f32[3,32,1]{2,1,0:T(8,128)S(1)} collective-permute-done((f32[3,32,1]{2,1,0:T(8,128)S(1)}, f32[3,32,1]{2,1,0:T(8,128)S(1)}, u32[]{:S(2)}, u32[]{:S(2)}) %collective-permute-start.5) | collective-permute-done | bytes 416 | tf_op jit(solution)/shard_map/ppermute | solution.py:26
  45.9 4.1 %collective-permute-start.3 = (f32[3,1,128]{2,1,0:T(1,128)S(1)}, f32[3,1,128]{2,1,0:T(1,128)S(1)}, u32[]{:S(2)}, u32[]{:S(2)}) collective-permute-start(f32[3,1,128]{2,1,0:T(1,128)S(1)} %get-tuple-element.45), channel_id=1, source_target_pairs={{4,0},{8,4},{12,8},{16,12},{20,16},{24,20},{28,24},{5,1},{9,5},{13... | collective-permute-start | bytes 4616 | tf_op jit(solution)/shard_map/ppermute | solution.py:26
  50.9 5.8 %fusion.1 = bf16[512,4096]{0,1:T(8,128)(2,1)S(1)} fusion(f32[4096,512]{1,0:T(8,128)} %get-tuple-element.53, bf16[3,4096]{1,0:T(4,128)(2,1)S(1)} %fusion.53, f32[3,512]{1,0:T(4,128)S(1)} %copy-done.12), kind=kOutput, calls=%fused_computation.3 | convolution fusion | flops 31458816 | bytes 12613632 | tf_op jit(solution)/shard_map/dot_general | solution.py:90
  56.7 3.3 %fusion.135.mid_ref = f32[512,512]{1,0:T(8,128)} fusion(bf16[512,4096]{0,1:T(8,128)(2,1)S(1)} %fusion.1, bf16[512,4096]{0,1:T(8,128)(2,1)S(1)} %copy-done.1), kind=kOutput, calls=%fused_computation.229 | convolution fusion | flops 2147483648 | bytes 9437184 | tf_op jit(solution)/shard_map/dot_general | solution.py:96
  60.0 3.6 %fusion = bf16[512,4096]{0,1:T(8,128)(2,1)S(1)} fusion(f32[4096,512]{1,0:T(8,128)S(1)} %bitcast.230, bf16[512,4096]{0,1:T(8,128)(2,1)S(1)} %fusion.1, f32[1,512,512]{2,1,0:T(8,128)S(1)} %copy-done.13), kind=kOutput, calls=%fused_computation.1 | convolution fusion | flops 2166620160 | bytes 17825792 | tf_op jit(solution)/shard_map/dot_general | solution.py:90
  63.6 1.4 convolution_bitcast_fusion
  69.4 6.2 %collective-permute-start.6 = (f32[32,42,1]{1,0,2:T(8,128)S(1)}, f32[32,42,1]{1,0,2:T(8,128)S(1)}, u32[]{:S(2)}, u32[]{:S(2)}) collective-permute-start(f32[32,42,1]{1,0,2:T(8,128)S(1)} %pad_maximum_fusion.8), channel_id=1, source_target_pairs={{0,1},{1,2},{2,3},{4,5},{5,6},{6,7},{8,9},{9,10},{10,11},{12,13},{... | collective-permute-start | bytes 16136 | tf_op jit(solution)/shard_map/ppermute | solution.py:26
  75.6 3.6 %fusion.136 = f32[512,64]{1,0:T(8,128)S(1)} fusion(bf16[512,4096]{0,1:T(8,128)(2,1)} %copy-done.3, bf16[64,4096]{1,0:T(8,128)(2,1)} %copy-done.10), kind=kOutput, calls=%fused_computation.230 | convolution fusion | flops 268435456 | bytes 4849664 | tf_op jit(solution)/shard_map/dot_general | solution.py:96
  81.2 1.5 %collective-permute-start.7 = (f32[32,1,160]{2,1,0:T(1,128)S(1)}, f32[32,1,160]{2,1,0:T(1,128)S(1)}, u32[]{:S(2)}, u32[]{:S(2)}) collective-permute-start(f32[32,1,160]{2,1,0:T(1,128)S(1)} %fusion.74), channel_id=1, source_target_pairs={{0,4},{4,8},{8,12},{12,16},{16,20},{20,24},{24,28},{1,5},{5,9},{9,... | collective-permute-start | bytes 61448 | tf_op jit(solution)/shard_map/ppermute | solution.py:26
  82.7 3.5 %fusion.137 = f32[512,3]{1,0:T(8,128)S(1)} fusion(bf16[512,4096]{0,1:T(8,128)(2,1)} %copy-done.2, bf16[3,4096]{1,0:T(4,128)(2,1)} %copy-done.11), kind=kOutput, calls=%fused_computation.231 | convolution fusion | flops 12582912 | bytes 4225024 | tf_op jit(solution)/shard_map/dot_general | solution.py:96
  90.3 46.6 %shard_map.200 = (f32[512,512]{1,0:T(8,128)}, f32[512,128]{1,0:T(8,128)}, f32[8,128]{1,0:T(8,128)}) custom-call(f32[512,512]{1,0:T(8,128)} %fusion.135.mid_ref, f32[512,128]{1,0:T(8,128)} %maximum_maximum_fusion.rest_ref, f32[512,512]{1,0:T(8,128)} %bitcast.220, f32[512,512]{1,0:T(8,128)} %bitcast.221, f32[512,128]{1,0:T(8,128)} %get-tuple-element.64.rest_first_ref, ...), custom_call_target="tpu_custom_call" | custom-call | tf_op jit(solution)/shard_map/pallas_call | solution.py:322
  137.0 1.3 slice.193
  140.8 1.7 %copy.126 = f32[512,64]{0,1:T(8,128)} copy(f32[512,64]{1,0:T(8,128)} %bitcast.215) | data formatting | bytes 262144
  142.5 2.3 %fusion.24 = f32[32,32,128]{2,1,0:T(8,128)} fusion(f32[32,32,128]{2,1,0:T(8,128)S(1)} %copy-done.6, f32[32,32,128]{2,1,0:T(8,128)} %param.24, f32[]{:T(128)} %bitcast.26, f32[32,33,127]{2,1,0:T(8,128)S(1)} %slice.229, f32[32,33,1]{2,1,0:T(8,128)S(1)} %copy.115, f32[32,1,128]{2,1,0:T(1,128)S(1)} %slice_add_fusion.1), kind=kLoop, calls=%fused_computation.39 | loop fusion | flops 2228224 | bytes 2129924 | tf_op jit(solution)/shard_map/div | solution.py:145
  (130 shorter events, 28.8 us)
Async XLA Ops:
  0.6 13.1 %copy-start.4 = (f32[32,32,128]{2,1,0:T(8,128)S(1)}, f32[32,32,128]{2,1,0:T(8,128)}, u32[]{:S(2)}) copy-start(f32[32,32,128]{2,1,0:T(8,128)} %param.19) | copy-start | bytes 1572868
  2.6 10.7 %collective-permute-start = (f32[32,1,160]{2,1,0:T(1,128)S(1)}, f32[32,1,160]{2,1,0:T(1,128)S(1)}, u32[]{:S(2)}, u32[]{:S(2)}) collective-permute-start(f32[32,1,160]{2,1,0:T(1,128)S(1)} %copy.103), channel_id=1, source_target_pairs={{4,0},{8,4},{12,8},{16,12},{20,16},{24,20},{28,24},{5,1},{9,5},{13... | collective-permute-start | bytes 61448 | tf_op jit(solution)/shard_map/ppermute | solution.py:26
  13.3 10.0 %copy-start.7 = (f32[512,64]{0,1:T(8,128)S(1)}, f32[512,64]{0,1:T(8,128)}, u32[]{:S(2)}) copy-start(f32[512,64]{0,1:T(8,128)} %param.21) | copy-start | bytes 393220
  14.2 5.4 %collective-permute-start.1 = (f32[32,42,1]{1,0,2:T(8,128)S(1)}, f32[32,42,1]{1,0,2:T(8,128)S(1)}, u32[]{:S(2)}, u32[]{:S(2)}) collective-permute-start(f32[32,42,1]{1,0,2:T(8,128)S(1)} %pad_maximum_fusion.7), channel_id=1, source_target_pairs={{1,0},{2,1},{3,2},{5,4},{6,5},{7,6},{9,8},{10,9},{11,10},{13,12},{... | collective-permute-start | bytes 16136 | tf_op jit(solution)/shard_map/ppermute | solution.py:26
  23.3 4.6 %copy-start.10 = (bf16[64,4096]{1,0:T(8,128)(2,1)}, bf16[64,4096]{1,0:T(8,128)(2,1)S(1)}, u32[]{:S(2)}) copy-start(bf16[64,4096]{1,0:T(8,128)(2,1)S(1)} %bitcast_dynamic-update-slice_fusion) | copy-start | bytes 1572868
  23.3 4.6 %copy-start.13 = (f32[1,512,512]{2,1,0:T(8,128)S(1)}, f32[1,512,512]{2,1,0:T(8,128)}, u32[]{:S(2)}) copy-start(f32[1,512,512]{2,1,0:T(8,128)} %param.22) | copy-start | bytes 3145732
  27.9 4.6 %copy-start = (bf16[512,4096]{0,1:T(8,128)(2,1)}, bf16[512,4096]{0,1:T(8,128)(2,1)S(1)}, u32[]{:S(2)}) copy-start(bf16[512,4096]{0,1:T(8,128)(2,1)S(1)} %get-tuple-element.50) | copy-start | bytes 12582916
  27.9 6.6 %copy-start.12 = (f32[3,512]{1,0:T(4,128)S(1)}, f32[3,512]{1,0:T(4,128)}, u32[]{:S(2)}) copy-start(f32[3,512]{1,0:T(4,128)} %param.23) | copy-start | bytes 18436
  32.6 2.0 %copy-start.2 = (bf16[512,4096]{0,1:T(8,128)(2,1)}, bf16[512,4096]{0,1:T(8,128)(2,1)S(1)}, u32[]{:S(2)}) copy-start(bf16[512,4096]{0,1:T(8,128)(2,1)S(1)} %get-tuple-element.52) | copy-start | bytes 12582916
  35.8 3.6 %collective-permute-start.4 = (f32[6,32,1]{2,1,0:T(8,128)S(1)}, f32[6,32,1]{2,1,0:T(8,128)S(1)}, u32[]{:S(2)}, u32[]{:S(2)}) collective-permute-start(f32[6,32,1]{2,1,0:T(8,128)S(1)} %pad_maximum_fusion.2), channel_id=1, source_target_pairs={{0,1},{1,2},{2,3},{4,5},{5,6},{6,7},{8,9},{9,10},{10,11},{12,13},{... | collective-permute-start | bytes 2312 | tf_op jit(solution)/shard_map/ppermute | solution.py:26
  39.4 6.3 %collective-permute-start.5 = (f32[3,32,1]{2,1,0:T(8,128)S(1)}, f32[3,32,1]{2,1,0:T(8,128)S(1)}, u32[]{:S(2)}, u32[]{:S(2)}) collective-permute-start(f32[3,32,1]{2,1,0:T(8,128)S(1)} %get-tuple-element.47), channel_id=1, source_target_pairs={{1,0},{2,1},{3,2},{5,4},{6,5},{7,6},{9,8},{10,9},{11,10},{13,12},{... | collective-permute-start | bytes 1160 | tf_op jit(solution)/shard_map/ppermute | solution.py:26
  41.4 4.4 %collective-permute-start.2 = (f32[6,1,128]{2,1,0:T(1,128)S(1)}, f32[6,1,128]{2,1,0:T(1,128)S(1)}, u32[]{:S(2)}, u32[]{:S(2)}) collective-permute-start(f32[6,1,128]{2,1,0:T(1,128)S(1)} %pad_maximum_fusion.9), channel_id=1, source_target_pairs={{0,4},{4,8},{8,12},{12,16},{16,20},{20,24},{24,28},{1,5},{5,9},{9,... | collective-permute-start | bytes 9224 | tf_op jit(solution)/shard_map/ppermute | solution.py:26
  45.7 14.3 %slice-start = ((s8[8388608]{0:T(1024)(128)(4,1)}), s8[4194304]{0:T(1024)(128)(4,1)S(1)}, s32[]{:S(2)}) async-start(s8[8388608]{0:T(1024)(128)(4,1)} %bitcast.229), calls=%async_computation | async-start | bytes 8388608
  45.9 4.6 %collective-permute-start.3 = (f32[3,1,128]{2,1,0:T(1,128)S(1)}, f32[3,1,128]{2,1,0:T(1,128)S(1)}, u32[]{:S(2)}, u32[]{:S(2)}) collective-permute-start(f32[3,1,128]{2,1,0:T(1,128)S(1)} %get-tuple-element.45), channel_id=1, source_target_pairs={{4,0},{8,4},{12,8},{16,12},{20,16},{24,20},{28,24},{5,1},{9,5},{13... | collective-permute-start | bytes 4616 | tf_op jit(solution)/shard_map/ppermute | solution.py:26
  50.9 5.8 %copy-start.11 = (bf16[3,4096]{1,0:T(4,128)(2,1)}, bf16[3,4096]{1,0:T(4,128)(2,1)S(1)}, u32[]{:S(2)}) copy-start(bf16[3,4096]{1,0:T(4,128)(2,1)S(1)} %fusion.53) | copy-start | bytes 73732
  50.9 5.8 %copy-start.1 = (bf16[512,4096]{0,1:T(8,128)(2,1)S(1)}, bf16[512,4096]{0,1:T(8,128)(2,1)}, u32[]{:S(2)}) copy-start(bf16[512,4096]{0,1:T(8,128)(2,1)} %copy-done) | copy-start | bytes 12582916
  50.9 9.1 %slice-start.1 = ((s8[8388608]{0:T(1024)(128)(4,1)}), s8[4194304]{0:T(1024)(128)(4,1)S(1)}, s32[]{:S(2)}) async-start(s8[8388608]{0:T(1024)(128)(4,1)} %bitcast.229), calls=%async_computation.1 | async-start | bytes 8388608
  63.6 2.0 %copy-start.3 = (bf16[512,4096]{0,1:T(8,128)(2,1)}, bf16[512,4096]{0,1:T(8,128)(2,1)S(1)}, u32[]{:S(2)}) copy-start(bf16[512,4096]{0,1:T(8,128)(2,1)S(1)} %fusion) | copy-start | bytes 12582916
  69.4 10.8 %collective-permute-start.6 = (f32[32,42,1]{1,0,2:T(8,128)S(1)}, f32[32,42,1]{1,0,2:T(8,128)S(1)}, u32[]{:S(2)}, u32[]{:S(2)}) collective-permute-start(f32[32,42,1]{1,0,2:T(8,128)S(1)} %pad_maximum_fusion.8), channel_id=1, source_target_pairs={{0,1},{1,2},{2,3},{4,5},{5,6},{6,7},{8,9},{9,10},{10,11},{12,13},{... | collective-permute-start | bytes 16136 | tf_op jit(solution)/shard_map/ppermute | solution.py:26
  81.2 5.2 %collective-permute-start.7 = (f32[32,1,160]{2,1,0:T(1,128)S(1)}, f32[32,1,160]{2,1,0:T(1,128)S(1)}, u32[]{:S(2)}, u32[]{:S(2)}) collective-permute-start(f32[32,1,160]{2,1,0:T(1,128)S(1)} %fusion.74), channel_id=1, source_target_pairs={{0,4},{4,8},{8,12},{12,16},{16,20},{20,24},{24,28},{1,5},{5,9},{9,... | collective-permute-start | bytes 61448 | tf_op jit(solution)/shard_map/ppermute | solution.py:26
  87.2 55.4 %copy-start.6 = (f32[32,32,128]{2,1,0:T(8,128)S(1)}, f32[32,32,128]{2,1,0:T(8,128)}, u32[]{:S(2)}) copy-start(f32[32,32,128]{2,1,0:T(8,128)} %param.25) | copy-start | bytes 1572868
  90.3 54.5 %copy-start.8 = (f32[32,8,32]{2,1,0:T(8,128)S(1)}, f32[32,8,32]{2,1,0:T(8,128)}, u32[]{:S(2)}) copy-start(f32[32,8,32]{2,1,0:T(8,128)} %param.27) | copy-start | bytes 98308
  90.3 54.5 %copy-start.9 = (f32[32,8,32]{2,1,0:T(8,128)S(1)}, f32[32,8,32]{2,1,0:T(8,128)}, u32[]{:S(2)}) copy-start(f32[32,8,32]{2,1,0:T(8,128)} %param.26) | copy-start | bytes 98308
  137.0 8.6 %copy-start.5 = (f32[512,512]{1,0:T(8,128)S(1)}, f32[512,512]{1,0:T(8,128)}, u32[]{:S(2)}) copy-start(f32[512,512]{1,0:T(8,128)} %get-tuple-element.10) | copy-start | bytes 3145732

commit v3 on v2

--- a/solution.py
+++ b/solution.py
@@ -157,8 +157,8 @@
     used,
     mid_ref,
     rest_ref,
-    mid_first_ref,
-    mid_second_ref,
+    mid_first_hbm,
+    mid_second_hbm,
     rest_first_ref,
     rest_second_ref,
     mid_step_ref,
@@ -174,6 +174,9 @@
     pair_recv,
     send,
     recv,
+    mid_first_ref,
+    mid_second_ref,
+    load_sem,
 ):
     row, col = lax.axis_index("row"), lax.axis_index("col")
     chips = mine_ref.shape[1]
@@ -226,6 +229,12 @@
         _, device = place(step)
         pl.semaphore_signal(barrier, inc=1, device_id=device, device_id_type=MESH)
 
+    loads = (
+        pltpu.make_async_copy(mid_first_hbm, mid_first_ref, load_sem.at[0]),
+        pltpu.make_async_copy(mid_second_hbm, mid_second_ref, load_sem.at[1]),
+    )
+    for load in loads:
+        load.start()
     hidden, mids = mid_ref.shape
     rows, lanes = mine_ref.shape[2:]
     rests = lanes - mids
@@ -272,6 +281,8 @@
     last.start()
     last.wait()
 
+    for load in loads:
+        load.wait()
     total_ref[...] = sum_ref[0, 0, :SUBLANES, mids:]
     kept = lax.broadcasted_iota(jnp.int32, (rows, rests), 1) < used
     mid_squares = jnp.zeros((rows, mids), jnp.float32)
@@ -322,7 +333,9 @@
     mid_step, rest_step, total = pl.pallas_call(
         functools.partial(decoder_kernel, used),
         out_shape=(flat, side, jax.ShapeDtypeStruct((SUBLANES, rests), jnp.float32)),
-        in_specs=[pl.BlockSpec(memory_space=pltpu.VMEM)] * 6,
+        in_specs=[
+            pl.BlockSpec(memory_space=pl.ANY if place in (2, 3) else pltpu.VMEM) for place in range(6)
+        ],
         out_specs=(pl.BlockSpec(memory_space=pltpu.VMEM),) * 3,
         scratch_shapes=[
             pltpu.VMEM(shape, jnp.float32),
@@ -335,6 +348,9 @@
             pltpu.SemaphoreType.DMA((2,)),
             pltpu.SemaphoreType.DMA((2, chips)),
             pltpu.SemaphoreType.DMA((2, chips)),
+            pltpu.VMEM((hidden, mids), jnp.float32),
+            pltpu.VMEM((hidden, mids), jnp.float32),
+            pltpu.SemaphoreType.DMA((2,)),
         ],
         compiler_params=pltpu.CompilerParams(collective_id=0, has_side_effects=True),
     )(

time: 147 us -> 147 us (level)
  no operation moved by 1% of the time
where the time goes in v3:
time: 147 us; the launch traced here: 146 us
  Pallas kernels  46 us (31%)
  matrix products  36.9 us (25%)
  starting transfers between devices  21.9 us (15%)
  local copies, waits for them, and re-layouts  21.1 us (14%)
  other arithmetic  7.81 us (5%)
  waiting for transfers between devices  7.59 us (5%)
  between operations  4.54 us (3%)
    pallas_call x1, Pallas kernels, decoder_steps(): pl.pallas_call(functools.partial(decoder_kernel, used), out_shape=(flat,...  46 us
    ppermute x8, starting transfers between devices, shifted(): return lax.ppermute(block, axis, route)  21.9 us
    unnamed x47, local copies, waits for them, and re-layouts  12 us
    dot_general x3, matrix products, contract_rows(): lax.dot_general(former, latter, (((0,), (0,)), ((), ())), preferred_eleme...  10.7 us
    dot_general x3, matrix products, matmul(): return jnp.dot(former, latter, preferred_element_type=jnp.float32)  10.4 us
    dot_general x3, matrix products, contract_cols(): lax.dot_general(former, latter, (((1,), (1,)), ((), ())), preferred_eleme...  10.4 us
    ppermute x8, waiting for transfers between devices, shifted(): return lax.ppermute(block, axis, route)  7.59 us
    div x2, other arithmetic, adam_step(): new_one / (1.0 - BETA_ONE ** ADAM_STEP)  3.06 us
  transfers between devices with their start and end apart: 8, of which 5 were waited for; matrix products, arithmetic and copies ran while one was open for 11% of the time, Pallas kernels for 0%

profile of v3, /device:TPU:27, one launch (start us, length us, event | category | flops | bytes accessed | tf_op | source)
XLA Modules:
  0.0 146.0 jit_solution(13654999486104871175)
XLA Ops:
  2.6 2.2 %collective-permute-start = (f32[32,1,160]{2,1,0:T(1,128)S(1)}, f32[32,1,160]{2,1,0:T(1,128)S(1)}, u32[]{:S(2)}, u32[]{:S(2)}) collective-permute-start(f32[32,1,160]{2,1,0:T(1,128)S(1)} %copy.103), channel_id=1, source_target_pairs={{4,0},{8,4},{12,8},{16,12},{20,16},{24,20},{28,24},{5,1},{9,5},{13... | collective-permute-start | bytes 61448 | tf_op jit(solution)/shard_map/ppermute | solution.py:26
  4.8 1.3 fusion.134
  14.2 2.9 %collective-permute-start.1 = (f32[32,42,1]{1,0,2:T(8,128)S(1)}, f32[32,42,1]{1,0,2:T(8,128)S(1)}, u32[]{:S(2)}, u32[]{:S(2)}) collective-permute-start(f32[32,42,1]{1,0,2:T(8,128)S(1)} %pad_maximum_fusion.7), channel_id=1, source_target_pairs={{1,0},{2,1},{3,2},{5,4},{6,5},{7,6},{9,8},{10,9},{11,10},{13,12},{... | collective-permute-start | bytes 16136 | tf_op jit(solution)/shard_map/ppermute | solution.py:26
  17.1 2.4 %collective-permute-done.1 = f32[32,42,1]{1,0,2:T(8,128)S(1)} collective-permute-done((f32[32,42,1]{1,0,2:T(8,128)S(1)}, f32[32,42,1]{1,0,2:T(8,128)S(1)}, u32[]{:S(2)}, u32[]{:S(2)}) %collective-permute-start.1) | collective-permute-done | bytes 5408 | tf_op jit(solution)/shard_map/ppermute | solution.py:26
  23.3 4.6 %fusion.11 = (bf16[512,4096]{0,1:T(8,128)(2,1)S(1)}, f32[4096,512]{1,0:T(8,128)}) fusion(bf16[64,4096]{1,0:T(8,128)(2,1)S(1)} %bitcast_dynamic-update-slice_fusion, f32[512,64]{0,1:T(8,128)S(1)} %copy-done.7), kind=kOutput, calls=%fused_computation.19 | convolution fusion | flops 278953984 | bytes 13238272 | tf_op jit(solution)/shard_map/dot_general | solution.py:86
  27.9 4.6 %fusion.5 = (bf16[512,4096]{0,1:T(8,128)(2,1)S(1)}, f32[4096,512]{1,0:T(8,128)}) fusion(bf16[512,4096]{0,1:T(8,128)(2,1)S(1)} %get-tuple-element.50, f32[1,512,512]{2,1,0:T(8,128)S(1)} %copy-done.13), kind=kOutput, calls=%fused_computation.10 | convolution fusion | flops 2158231552 | bytes 17825792 | tf_op jit(solution)/shard_map/dot_general | solution.py:86
  32.6 2.0 %copy-done.2 = bf16[512,4096]{0,1:T(8,128)(2,1)} copy-done((bf16[512,4096]{0,1:T(8,128)(2,1)}, bf16[512,4096]{0,1:T(8,128)(2,1)S(1)}, u32[]{:S(2)}) %copy-start.2) | copy-done | bytes 4194328
  35.8 1.9 %collective-permute-start.4 = (f32[6,32,1]{2,1,0:T(8,128)S(1)}, f32[6,32,1]{2,1,0:T(8,128)S(1)}, u32[]{:S(2)}, u32[]{:S(2)}) collective-permute-start(f32[6,32,1]{2,1,0:T(8,128)S(1)} %pad_maximum_fusion.2), channel_id=1, source_target_pairs={{0,1},{1,2},{2,3},{4,5},{5,6},{6,7},{8,9},{9,10},{10,11},{12,13},{... | collective-permute-start | bytes 2312 | tf_op jit(solution)/shard_map/ppermute | solution.py:26
  37.9 1.5 %collective-permute-done.4 = f32[6,32,1]{2,1,0:T(8,128)S(1)} collective-permute-done((f32[6,32,1]{2,1,0:T(8,128)S(1)}, f32[6,32,1]{2,1,0:T(8,128)S(1)}, u32[]{:S(2)}, u32[]{:S(2)}) %collective-permute-start.4) | collective-permute-done | bytes 800 | tf_op jit(solution)/shard_map/ppermute | solution.py:26
  39.4 1.9 %collective-permute-start.5 = (f32[3,32,1]{2,1,0:T(8,128)S(1)}, f32[3,32,1]{2,1,0:T(8,128)S(1)}, u32[]{:S(2)}, u32[]{:S(2)}) collective-permute-start(f32[3,32,1]{2,1,0:T(8,128)S(1)} %get-tuple-element.47), channel_id=1, source_target_pairs={{1,0},{2,1},{3,2},{5,4},{6,5},{7,6},{9,8},{10,9},{11,10},{13,12},{... | collective-permute-start | bytes 1160 | tf_op jit(solution)/shard_map/ppermute | solution.py:26
  42.7 3.0 %collective-permute-done.5 = f32[3,32,1]{2,1,0:T(8,128)S(1)} collective-permute-done((f32[3,32,1]{2,1,0:T(8,128)S(1)}, f32[3,32,1]{2,1,0:T(8,128)S(1)}, u32[]{:S(2)}, u32[]{:S(2)}) %collective-permute-start.5) | collective-permute-done | bytes 416 | tf_op jit(solution)/shard_map/ppermute | solution.py:26
  45.9 4.1 %collective-permute-start.3 = (f32[3,1,128]{2,1,0:T(1,128)S(1)}, f32[3,1,128]{2,1,0:T(1,128)S(1)}, u32[]{:S(2)}, u32[]{:S(2)}) collective-permute-start(f32[3,1,128]{2,1,0:T(1,128)S(1)} %get-tuple-element.45), channel_id=1, source_target_pairs={{4,0},{8,4},{12,8},{16,12},{20,16},{24,20},{28,24},{5,1},{9,5},{13... | collective-permute-start | bytes 4616 | tf_op jit(solution)/shard_map/ppermute | solution.py:26
  50.9 5.8 %fusion.1 = bf16[512,4096]{0,1:T(8,128)(2,1)S(1)} fusion(f32[4096,512]{1,0:T(8,128)} %get-tuple-element.53, bf16[3,4096]{1,0:T(4,128)(2,1)S(1)} %fusion.53, f32[3,512]{1,0:T(4,128)S(1)} %copy-done.12), kind=kOutput, calls=%fused_computation.3 | convolution fusion | flops 31458816 | bytes 12613632 | tf_op jit(solution)/shard_map/dot_general | solution.py:90
  56.7 3.3 %fusion.135.mid_ref = f32[512,512]{1,0:T(8,128)} fusion(bf16[512,4096]{0,1:T(8,128)(2,1)S(1)} %fusion.1, bf16[512,4096]{0,1:T(8,128)(2,1)S(1)} %copy-done.1), kind=kOutput, calls=%fused_computation.229 | convolution fusion | flops 2147483648 | bytes 9437184 | tf_op jit(solution)/shard_map/dot_general | solution.py:96
  60.0 3.6 %fusion = bf16[512,4096]{0,1:T(8,128)(2,1)S(1)} fusion(f32[4096,512]{1,0:T(8,128)S(1)} %bitcast.230, bf16[512,4096]{0,1:T(8,128)(2,1)S(1)} %fusion.1, f32[1,512,512]{2,1,0:T(8,128)S(1)} %copy-done.13), kind=kOutput, calls=%fused_computation.1 | convolution fusion | flops 2166620160 | bytes 17825792 | tf_op jit(solution)/shard_map/dot_general | solution.py:90
  63.6 1.4 convolution_bitcast_fusion
  69.4 6.2 %collective-permute-start.6 = (f32[32,42,1]{1,0,2:T(8,128)S(1)}, f32[32,42,1]{1,0,2:T(8,128)S(1)}, u32[]{:S(2)}, u32[]{:S(2)}) collective-permute-start(f32[32,42,1]{1,0,2:T(8,128)S(1)} %pad_maximum_fusion.8), channel_id=1, source_target_pairs={{0,1},{1,2},{2,3},{4,5},{5,6},{6,7},{8,9},{9,10},{10,11},{12,13},{... | collective-permute-start | bytes 16136 | tf_op jit(solution)/shard_map/ppermute | solution.py:26
  75.6 3.6 %fusion.136 = f32[512,64]{1,0:T(8,128)S(1)} fusion(bf16[512,4096]{0,1:T(8,128)(2,1)} %copy-done.3, bf16[64,4096]{1,0:T(8,128)(2,1)} %copy-done.10), kind=kOutput, calls=%fused_computation.230 | convolution fusion | flops 268435456 | bytes 4849664 | tf_op jit(solution)/shard_map/dot_general | solution.py:96
  81.2 1.5 %collective-permute-start.7 = (f32[32,1,160]{2,1,0:T(1,128)S(1)}, f32[32,1,160]{2,1,0:T(1,128)S(1)}, u32[]{:S(2)}, u32[]{:S(2)}) collective-permute-start(f32[32,1,160]{2,1,0:T(1,128)S(1)} %fusion.74), channel_id=1, source_target_pairs={{0,4},{4,8},{8,12},{12,16},{16,20},{20,24},{24,28},{1,5},{5,9},{9,... | collective-permute-start | bytes 61448 | tf_op jit(solution)/shard_map/ppermute | solution.py:26
  82.7 3.5 %fusion.137 = f32[512,3]{1,0:T(8,128)S(1)} fusion(bf16[512,4096]{0,1:T(8,128)(2,1)} %copy-done.2, bf16[3,4096]{1,0:T(4,128)(2,1)} %copy-done.11), kind=kOutput, calls=%fused_computation.231 | convolution fusion | flops 12582912 | bytes 4225024 | tf_op jit(solution)/shard_map/dot_general | solution.py:96
  90.3 46.0 %shard_map.200 = (f32[512,512]{1,0:T(8,128)}, f32[512,128]{1,0:T(8,128)}, f32[8,128]{1,0:T(8,128)}) custom-call(f32[512,512]{1,0:T(8,128)} %fusion.135.mid_ref, f32[512,128]{1,0:T(8,128)} %maximum_maximum_fusion.rest_ref, f32[512,512]{1,0:T(8,128)} %bitcast.220, f32[512,512]{1,0:T(8,128)} %bitcast.221, f32[512,128]{1,0:T(8,128)} %get-tuple-element.64.rest_first_ref, ...), custom_call_target="tpu_custom_call" | custom-call | tf_op jit(solution)/shard_map/pallas_call | solution.py:333
  136.4 1.3 slice.193
  140.2 1.7 %copy.126 = f32[512,64]{0,1:T(8,128)} copy(f32[512,64]{1,0:T(8,128)} %bitcast.215) | data formatting | bytes 262144
  141.9 2.3 %fusion.24 = f32[32,32,128]{2,1,0:T(8,128)} fusion(f32[32,32,128]{2,1,0:T(8,128)S(1)} %copy-done.6, f32[32,32,128]{2,1,0:T(8,128)} %param.24, f32[]{:T(128)} %bitcast.26, f32[32,33,127]{2,1,0:T(8,128)S(1)} %slice.229, f32[32,33,1]{2,1,0:T(8,128)S(1)} %copy.115, f32[32,1,128]{2,1,0:T(1,128)S(1)} %slice_add_fusion.1), kind=kLoop, calls=%fused_computation.39 | loop fusion | flops 2228224 | bytes 2129924 | tf_op jit(solution)/shard_map/div | solution.py:145
  (130 shorter events, 28.8 us)
Async XLA Ops:
  0.6 13.1 %copy-start.4 = (f32[32,32,128]{2,1,0:T(8,128)S(1)}, f32[32,32,128]{2,1,0:T(8,128)}, u32[]{:S(2)}) copy-start(f32[32,32,128]{2,1,0:T(8,128)} %param.19) | copy-start | bytes 1572868
  2.6 10.7 %collective-permute-start = (f32[32,1,160]{2,1,0:T(1,128)S(1)}, f32[32,1,160]{2,1,0:T(1,128)S(1)}, u32[]{:S(2)}, u32[]{:S(2)}) collective-permute-start(f32[32,1,160]{2,1,0:T(1,128)S(1)} %copy.103), channel_id=1, source_target_pairs={{4,0},{8,4},{12,8},{16,12},{20,16},{24,20},{28,24},{5,1},{9,5},{13... | collective-permute-start | bytes 61448 | tf_op jit(solution)/shard_map/ppermute | solution.py:26
  13.3 10.0 %copy-start.7 = (f32[512,64]{0,1:T(8,128)S(1)}, f32[512,64]{0,1:T(8,128)}, u32[]{:S(2)}) copy-start(f32[512,64]{0,1:T(8,128)} %param.21) | copy-start | bytes 393220
  14.2 5.4 %collective-permute-start.1 = (f32[32,42,1]{1,0,2:T(8,128)S(1)}, f32[32,42,1]{1,0,2:T(8,128)S(1)}, u32[]{:S(2)}, u32[]{:S(2)}) collective-permute-start(f32[32,42,1]{1,0,2:T(8,128)S(1)} %pad_maximum_fusion.7), channel_id=1, source_target_pairs={{1,0},{2,1},{3,2},{5,4},{6,5},{7,6},{9,8},{10,9},{11,10},{13,12},{... | collective-permute-start | bytes 16136 | tf_op jit(solution)/shard_map/ppermute | solution.py:26
  23.3 4.6 %copy-start.10 = (bf16[64,4096]{1,0:T(8,128)(2,1)}, bf16[64,4096]{1,0:T(8,128)(2,1)S(1)}, u32[]{:S(2)}) copy-start(bf16[64,4096]{1,0:T(8,128)(2,1)S(1)} %bitcast_dynamic-update-slice_fusion) | copy-start | bytes 1572868
  23.3 4.6 %copy-start.13 = (f32[1,512,512]{2,1,0:T(8,128)S(1)}, f32[1,512,512]{2,1,0:T(8,128)}, u32[]{:S(2)}) copy-start(f32[1,512,512]{2,1,0:T(8,128)} %param.22) | copy-start | bytes 3145732
  27.9 4.6 %copy-start = (bf16[512,4096]{0,1:T(8,128)(2,1)}, bf16[512,4096]{0,1:T(8,128)(2,1)S(1)}, u32[]{:S(2)}) copy-start(bf16[512,4096]{0,1:T(8,128)(2,1)S(1)} %get-tuple-element.50) | copy-start | bytes 12582916
  27.9 6.6 %copy-start.12 = (f32[3,512]{1,0:T(4,128)S(1)}, f32[3,512]{1,0:T(4,128)}, u32[]{:S(2)}) copy-start(f32[3,512]{1,0:T(4,128)} %param.23) | copy-start | bytes 18436
  32.6 2.0 %copy-start.2 = (bf16[512,4096]{0,1:T(8,128)(2,1)}, bf16[512,4096]{0,1:T(8,128)(2,1)S(1)}, u32[]{:S(2)}) copy-start(bf16[512,4096]{0,1:T(8,128)(2,1)S(1)} %get-tuple-element.52) | copy-start | bytes 12582916
  35.8 3.6 %collective-permute-start.4 = (f32[6,32,1]{2,1,0:T(8,128)S(1)}, f32[6,32,1]{2,1,0:T(8,128)S(1)}, u32[]{:S(2)}, u32[]{:S(2)}) collective-permute-start(f32[6,32,1]{2,1,0:T(8,128)S(1)} %pad_maximum_fusion.2), channel_id=1, source_target_pairs={{0,1},{1,2},{2,3},{4,5},{5,6},{6,7},{8,9},{9,10},{10,11},{12,13},{... | collective-permute-start | bytes 2312 | tf_op jit(solution)/shard_map/ppermute | solution.py:26
  39.4 6.3 %collective-permute-start.5 = (f32[3,32,1]{2,1,0:T(8,128)S(1)}, f32[3,32,1]{2,1,0:T(8,128)S(1)}, u32[]{:S(2)}, u32[]{:S(2)}) collective-permute-start(f32[3,32,1]{2,1,0:T(8,128)S(1)} %get-tuple-element.47), channel_id=1, source_target_pairs={{1,0},{2,1},{3,2},{5,4},{6,5},{7,6},{9,8},{10,9},{11,10},{13,12},{... | collective-permute-start | bytes 1160 | tf_op jit(solution)/shard_map/ppermute | solution.py:26
  41.4 4.4 %collective-permute-start.2 = (f32[6,1,128]{2,1,0:T(1,128)S(1)}, f32[6,1,128]{2,1,0:T(1,128)S(1)}, u32[]{:S(2)}, u32[]{:S(2)}) collective-permute-start(f32[6,1,128]{2,1,0:T(1,128)S(1)} %pad_maximum_fusion.9), channel_id=1, source_target_pairs={{0,4},{4,8},{8,12},{12,16},{16,20},{20,24},{24,28},{1,5},{5,9},{9,... | collective-permute-start | bytes 9224 | tf_op jit(solution)/shard_map/ppermute | solution.py:26
  45.7 14.3 %slice-start = ((s8[8388608]{0:T(1024)(128)(4,1)}), s8[4194304]{0:T(1024)(128)(4,1)S(1)}, s32[]{:S(2)}) async-start(s8[8388608]{0:T(1024)(128)(4,1)} %bitcast.229), calls=%async_computation | async-start | bytes 8388608
  45.9 4.6 %collective-permute-start.3 = (f32[3,1,128]{2,1,0:T(1,128)S(1)}, f32[3,1,128]{2,1,0:T(1,128)S(1)}, u32[]{:S(2)}, u32[]{:S(2)}) collective-permute-start(f32[3,1,128]{2,1,0:T(1,128)S(1)} %get-tuple-element.45), channel_id=1, source_target_pairs={{4,0},{8,4},{12,8},{16,12},{20,16},{24,20},{28,24},{5,1},{9,5},{13... | collective-permute-start | bytes 4616 | tf_op jit(solution)/shard_map/ppermute | solution.py:26
  50.9 5.8 %copy-start.11 = (bf16[3,4096]{1,0:T(4,128)(2,1)}, bf16[3,4096]{1,0:T(4,128)(2,1)S(1)}, u32[]{:S(2)}) copy-start(bf16[3,4096]{1,0:T(4,128)(2,1)S(1)} %fusion.53) | copy-start | bytes 73732
  50.9 5.8 %copy-start.1 = (bf16[512,4096]{0,1:T(8,128)(2,1)S(1)}, bf16[512,4096]{0,1:T(8,128)(2,1)}, u32[]{:S(2)}) copy-start(bf16[512,4096]{0,1:T(8,128)(2,1)} %copy-done) | copy-start | bytes 12582916
  50.9 9.1 %slice-start.1 = ((s8[8388608]{0:T(1024)(128)(4,1)}), s8[4194304]{0:T(1024)(128)(4,1)S(1)}, s32[]{:S(2)}) async-start(s8[8388608]{0:T(1024)(128)(4,1)} %bitcast.229), calls=%async_computation.1 | async-start | bytes 8388608
  63.6 2.0 %copy-start.3 = (bf16[512,4096]{0,1:T(8,128)(2,1)}, bf16[512,4096]{0,1:T(8,128)(2,1)S(1)}, u32[]{:S(2)}) copy-start(bf16[512,4096]{0,1:T(8,128)(2,1)S(1)} %fusion) | copy-start | bytes 12582916
  69.4 10.8 %collective-permute-start.6 = (f32[32,42,1]{1,0,2:T(8,128)S(1)}, f32[32,42,1]{1,0,2:T(8,128)S(1)}, u32[]{:S(2)}, u32[]{:S(2)}) collective-permute-start(f32[32,42,1]{1,0,2:T(8,128)S(1)} %pad_maximum_fusion.8), channel_id=1, source_target_pairs={{0,1},{1,2},{2,3},{4,5},{5,6},{6,7},{8,9},{9,10},{10,11},{12,13},{... | collective-permute-start | bytes 16136 | tf_op jit(solution)/shard_map/ppermute | solution.py:26
  81.2 5.2 %collective-permute-start.7 = (f32[32,1,160]{2,1,0:T(1,128)S(1)}, f32[32,1,160]{2,1,0:T(1,128)S(1)}, u32[]{:S(2)}, u32[]{:S(2)}) collective-permute-start(f32[32,1,160]{2,1,0:T(1,128)S(1)} %fusion.74), channel_id=1, source_target_pairs={{0,4},{4,8},{8,12},{12,16},{16,20},{20,24},{24,28},{1,5},{5,9},{9,... | collective-permute-start | bytes 61448 | tf_op jit(solution)/shard_map/ppermute | solution.py:26
  87.2 54.8 %copy-start.6 = (f32[32,32,128]{2,1,0:T(8,128)S(1)}, f32[32,32,128]{2,1,0:T(8,128)}, u32[]{:S(2)}) copy-start(f32[32,32,128]{2,1,0:T(8,128)} %param.25) | copy-start | bytes 1572868
  90.3 53.9 %copy-start.8 = (f32[32,8,32]{2,1,0:T(8,128)S(1)}, f32[32,8,32]{2,1,0:T(8,128)}, u32[]{:S(2)}) copy-start(f32[32,8,32]{2,1,0:T(8,128)} %param.27) | copy-start | bytes 98308
  90.3 53.9 %copy-start.9 = (f32[32,8,32]{2,1,0:T(8,128)S(1)}, f32[32,8,32]{2,1,0:T(8,128)}, u32[]{:S(2)}) copy-start(f32[32,8,32]{2,1,0:T(8,128)} %param.26) | copy-start | bytes 98308
  136.4 8.6 %copy-start.5 = (f32[512,512]{1,0:T(8,128)S(1)}, f32[512,512]{1,0:T(8,128)}, u32[]{:S(2)}) copy-start(f32[512,512]{1,0:T(8,128)} %get-tuple-element.10) | copy-start | bytes 3145732
